TPU v7x, 16 devices: a whole 2x2x2 slice. The times are simulated.
16 devices in a mesh: dp: 2 (over z), vp: 8 (over y, x, core).
Axes of the slice: x: 2, y: 2, z: 2, core: 2. Of those that a mesh axis runs over, the one named last changes fastest.
Arguments:
- hidden: bfloat16 [4096, 4096], P(('dp', 'vp')), parts along dimension 0
- labels: int32 [4096], P(('dp', 'vp')), parts along dimension 0
- loss_weight: float32 [4096], P(('dp', 'vp')), parts along dimension 0
- norm_gain: float32 [4096], replicated
- w_unembed: bfloat16 [4096, 32128], P(None, 'vp')
Outputs:
- output 1: float32 [2], P('dp'), parts along dimension 0
- output 2: bfloat16 [4096, 4096], P(('dp', 'vp')), parts along dimension 0
- output 3: float32 [8192, 32128], P('dp', 'vp'), parts along dimension 0
- output 4: float32 [8192], P('dp'), parts along dimension 0
There are 2 independent parts. A program takes and returns all parts, laid end to end along the dimension named above; an argument that names none is the same for every part.
All inputs are finite; a program needn't handle non-finite values.
Results may differ from a plain program's by a relative error of at most 0.001.
Values are sent between devices in bfloat16 or wider.
A program may use at most 1 GiB of HBM per device.

v0:
```python
import jax
import jax.numpy as jnp
from jax import lax
from jax.sharding import PartitionSpec as P

NORM_EPS = 1e-5
PAD_COLS = 128


def solution(mesh):
    group_size = mesh.shape["vp"]

    def local_step(hidden, labels, loss_weight, norm_gain, w_local):
        vocab_local = w_local.shape[1]
        vocab_real = vocab_local * group_size - PAD_COLS
        x_float = hidden.astype(jnp.float32)
        inv_rms = lax.rsqrt(jnp.mean(x_float * x_float, axis=-1, keepdims=True) + NORM_EPS)
        x_norm = x_float * inv_rms
        normed = (x_norm * norm_gain).astype(jnp.bfloat16)
        normed_all = lax.all_gather(normed, "vp", axis=0, tiled=True)
        labels_all = lax.all_gather(labels, "vp", axis=0, tiled=True)
        weights_all = lax.all_gather(loss_weight, "vp", axis=0, tiled=True)
        col_ids = lax.axis_index("vp") * vocab_local + lax.broadcasted_iota(jnp.int32, (1, vocab_local), 1)
        logits = jnp.dot(normed_all, w_local, preferred_element_type=jnp.float32)
        logits = jnp.where(col_ids < vocab_real, logits, -jnp.inf)
        is_target = col_ids == labels_all[:, None]
        row_max = lax.pmax(jnp.max(logits, axis=1), "vp")
        shifted = jnp.exp(logits - row_max[:, None])
        sum_exp = lax.psum(jnp.sum(shifted, axis=1), "vp")
        target = lax.psum(jnp.sum(jnp.where(is_target, logits, 0.0), axis=1), "vp")
        log_norm = row_max + jnp.log(sum_exp)
        tok_scale = weights_all / jnp.sum(weights_all)
        mean_loss = jnp.sum(tok_scale * (log_norm - target)).reshape(1)
        prob_all = shifted / sum_exp[:, None]
        d_logits = ((prob_all - jnp.where(is_target, 1.0, 0.0)) * tok_scale[:, None]).astype(jnp.bfloat16)
        d_unembed = lax.dot_general(normed_all, d_logits, (((0,), (0,)), ((), ())), preferred_element_type=jnp.float32)
        d_part = lax.dot_general(d_logits, w_local, (((1,), (1,)), ((), ())), preferred_element_type=jnp.float32)
        d_normed = lax.psum_scatter(d_part, "vp", scatter_dimension=0, tiled=True)
        grad_hat = d_normed * norm_gain
        d_input = inv_rms * (grad_hat - x_norm * jnp.mean(grad_hat * x_norm, axis=-1, keepdims=True))
        d_norm_gain = lax.psum(jnp.sum(d_normed * x_norm, axis=0), "vp")
        return mean_loss, d_input.astype(jnp.bfloat16), d_unembed, d_norm_gain

    return jax.shard_map(
        local_step,
        mesh=mesh,
        in_specs=(P(("dp", "vp"), None), P(("dp", "vp")), P(("dp", "vp")), P(None), P(None, "vp")),
        out_specs=(P("dp"), P(("dp", "vp"), None), P("dp", "vp"), P("dp")),
        check_vma=False,
    )
```

profile of v0, /device:TPU:0, one launch (start us, length us, event | category | flops | bytes accessed | tf_op | source)
XLA Modules:
  0.0 564.1 jit_solution(4886202511844632727)
XLA Ops:
  7.2 0.0 all-gather.4.cloned.1.call-start
  7.2 2.1 fusion.15
  9.3 0.6 copy-done.9
  9.9 3.5 fusion.9
  13.4 0.0 all-gather.4.cloned.1.call-update
  13.5 0.0 reduce-scatter.2.cloned.1.call-start
  13.5 10.7 %all-gather = f32[8,1,256]{2,1,0:T(1,128)S(1)} all-gather(f32[1,1,256]{2,1,0:T(1,128)} %bitcast.18), channel_id=1, replica_groups=mesh['dp'=2,'vp'=8] {'vp'}, dimensions={0}, use_global_device_ids=true | all-gather | bytes 9216 | tf_op jit(solution)/shard_map/all_gather | solution.py:22
  24.2 0.6 reduce_sum.63
  24.8 8.8 %all-gather.1 = s32[8,1,256]{2,1,0:T(1,128)S(1)} all-gather(s32[1,1,256]{2,1,0:T(1,128)} %bitcast.19), channel_id=1, replica_groups=mesh['dp'=2,'vp'=8] {'vp'}, dimensions={0}, use_global_device_ids=true | all-gather | bytes 9216 | tf_op jit(solution)/shard_map/all_gather | solution.py:21
  33.6 1.3 broadcast_divide_fusion
  34.9 67.6 %all-gather.4.cloned.1.call-done = bf16[2048,4096]{1,0:T(8,128)(2,1)} async-done(((bf16[256,4096]{1,0:T(8,128)(2,1)}), bf16[2048,4096]{1,0:T(8,128)(2,1)}) %all-gather.4.cloned.1.call-update) | async-done | bytes 16777232 | tf_op jit(solution)/shard_map/all_gather | solution.py:20
  102.4 80.0 %select_reduce_fusion = (f32[2048]{0:T(1024)S(1)}, f32[2048,4016]{0,1:T(8,128)}) fusion(pred[4016]{0:T(1024)(128)(4,1)S(1)} %broadcast_compare_fusion, bf16[2048,4096]{1,0:T(8,128)(2,1)} %all-gather.4.cloned.1.call-done, bf16[4096,4016]{0,1:T(8,128)(2,1)} %param.9), kind=kOutput, calls=%fused_computation.8 | convolution fusion | flops 67393748992 | bytes 82587568 | tf_op jit(solution)/shard_map/dot_general | solution.py:24
  182.4 13.5 %pmax.7 = f32[2048]{0:T(1024)S(1)} all-reduce(f32[2048]{0:T(1024)S(1)} %get-tuple-element.10), channel_id=1, replica_groups=mesh['dp'=2,'vp'=8] {'vp'}, use_global_device_ids=true, to_apply=%region_3.4 | all-reduce | flops 2048 | bytes 16384 | tf_op jit(solution)/shard_map/pmax | solution.py:27
  196.0 16.5 %fusion.4 = (f32[2048]{0:T(1024)S(1)}, f32[2048]{0:T(1024)}) fusion(f32[2048,4016]{0,1:T(8,128)} %get-tuple-element.11, f32[2048]{0:T(1024)S(1)} %pmax.7, pred[4016]{0:T(1024)(128)(4,1)S(1)} %broadcast_compare_fusion, s32[2048]{0:T(1024)S(1)} %bitcast.14, s32[4016]{0:T(1024)S(1)} %iota_add_fusion), kind=kLoop, calls=%fused_computation.7 | loop fusion | flops 49344512 | bytes 32951920 | tf_op jit(solution)/shard_map/reduce_sum | solution.py:29
  212.5 12.0 %psum.21 = f32[2048]{0:T(1024)S(1)} all-reduce(f32[2048]{0:T(1024)S(1)} %get-tuple-element.4), channel_id=1, replica_groups=mesh['dp'=2,'vp'=8] {'vp'}, use_global_device_ids=true, to_apply=%region_5.6 | all-reduce | flops 2048 | bytes 16384 | tf_op jit(solution)/shard_map/psum | solution.py:29
  224.5 22.0 %fusion.3 = bf16[2048,4016]{0,1:T(8,128)(2,1)} fusion(f32[2048,4016]{0,1:T(8,128)} %get-tuple-element.11, f32[2048]{0:T(1024)S(1)} %bitcast.16, f32[2048]{0:T(1024)S(1)} %psum.21, s32[2048]{0:T(1024)S(1)} %bitcast.15, f32[2048]{0:T(1024)S(1)} %pmax.7, s32[4016]{0:T(1024)S(1)} %iota_add_fusion, pred[4016]{0:T(1024)(128)(4,1)S(1)} %broadcast_compare_fusion), kind=kLoop, calls=%fused_computation.5 | loop fusion | flops 65798144 | bytes 49401456 | tf_op jit(solution)/shard_map/convert_element_type | solution.py:35
  246.6 79.3 %fusion.16 = f32[2048,4096]{1,0:T(8,128)} fusion(bf16[2048,4016]{0,1:T(8,128)(2,1)} %fusion.3, bf16[4096,4016]{0,1:T(8,128)(2,1)} %param.9), kind=kOutput, calls=%fused_computation.28 | convolution fusion | flops 67377299456 | bytes 82903040 | tf_op jit(solution)/shard_map/dot_general | solution.py:37
  325.9 0.0 reduce-scatter.2.cloned.1.call-update
  326.0 79.2 %fusion.17 = f32[4096,4016]{0,1:T(8,128)} fusion(bf16[2048,4016]{0,1:T(8,128)(2,1)} %fusion.3, bf16[2048,4096]{1,0:T(8,128)(2,1)} %all-gather.4.cloned.1.call-done), kind=kOutput, calls=%fused_computation.29 | convolution fusion | flops 67377299456 | bytes 99024896 | tf_op jit(solution)/shard_map/dot_general | solution.py:36
  405.2 119.9 %reduce-scatter.2.cloned.1.call-done = f32[256,4096]{1,0:T(8,128)} async-done(((f32[2048,4096]{1,0:T(8,128)}), f32[256,4096]{1,0:T(8,128)}) %reduce-scatter.2.cloned.1.call-update) | async-done | bytes 4194320 | tf_op jit(solution)/shard_map/reduce_scatter | solution.py:38
  525.1 3.4 fusion.14
  528.5 23.4 %all-reduce = (f32[2048]{0:T(1024)S(1)}, f32[4096]{0:T(1024)}) all-reduce(f32[2048]{0:T(1024)S(1)} %copy-done.8, f32[4096]{0:T(1024)S(1)} %get-tuple-element.6), channel_id=1, replica_groups=mesh['dp'=2,'vp'=8] {'vp'}, use_global_device_ids=true, to_apply=%region_7.8 | all-reduce | flops 6144 | bytes 49152 | tf_op jit(solution)/shard_map/psum | solution.py:30
  551.9 0.6 multiply_reduce_fusion
  552.6 4.7 fusion.13
  (25 shorter events, 0.1 us)
Async XLA Ops:
  7.2 95.3 %all-gather.4.cloned.1.call-start = ((), (), s32[]{:S(2)}) async-start(), calls=%async_computation.1 | async-start | bytes 18874368 | tf_op jit(solution)/shard_map/all_gather | solution.py:20
  9.3 0.6 copy-start.9
  13.5 511.6 %reduce-scatter.2.cloned.1.call-start = ((), (), s32[]{:S(2)}) async-start(), calls=%async_computation.2 | async-start | bytes 37748736 | tf_op jit(solution)/shard_map/reduce_scatter | solution.py:38
  182.4 42.1 %copy-start.4 = (f32[1,8,256]{2,1,0:T(8,128)S(1)}, f32[1,8,256]{2,1,0:T(8,128)}, u32[]{:S(2)}) copy-start(f32[1,8,256]{2,1,0:T(8,128)} %broadcast_divide_fusion) | copy-start | bytes 24580
  196.0 50.6 %copy-start.2 = (f32[2048]{0:T(1024)}, f32[2048]{0:T(1024)S(1)}, u32[]{:S(2)}) copy-start(f32[2048]{0:T(1024)S(1)} %pmax.7) | copy-start | bytes 24580
  224.5 22.0 %copy-start.6 = (f32[2048]{0:T(1024)}, f32[2048]{0:T(1024)S(1)}, u32[]{:S(2)}) copy-start(f32[2048]{0:T(1024)S(1)} %psum.21) | copy-start | bytes 24580
  325.9 199.2 %copy-start = (bf16[256,4096]{1,0:T(8,128)(2,1)S(1)}, bf16[256,4096]{1,0:T(8,128)(2,1)}, u32[]{:S(2)}) copy-start(bf16[256,4096]{1,0:T(8,128)(2,1)} %param.5) | copy-start | bytes 6291460
  325.9 199.2 %copy-start.1 = (f32[4096]{0:T(1024)S(1)}, f32[4096]{0:T(1024)}, u32[]{:S(2)}) copy-start(f32[4096]{0:T(1024)} %param.8) | copy-start | bytes 49156
  325.9 199.2 %copy-start.10 = (f32[256]{0:T(256)S(1)}, f32[256]{0:T(256)}, u32[]{:S(2)}) copy-start(f32[256]{0:T(256)} %copy-done.9) | copy-start | bytes 3076
  325.9 202.6 %copy-start.8 = (f32[2048]{0:T(1024)S(1)}, f32[2048]{0:T(1024)}, u32[]{:S(2)}) copy-start(f32[2048]{0:T(1024)} %get-tuple-element.5) | copy-start | bytes 24580
  325.9 226.0 %copy-start.3 = (f32[2048]{0:T(1024)S(1)}, f32[2048]{0:T(1024)}, u32[]{:S(2)}) copy-start(f32[2048]{0:T(1024)} %copy-done.2) | copy-start | bytes 24580
  325.9 226.0 %copy-start.5 = (f32[1,8,256]{2,1,0:T(8,128)S(1)}, f32[1,8,256]{2,1,0:T(8,128)}, u32[]{:S(2)}) copy-start(f32[1,8,256]{2,1,0:T(8,128)} %broadcast_divide_fusion) | copy-start | bytes 24580
  326.0 226.0 %copy-start.7 = (f32[2048]{0:T(1024)S(1)}, f32[2048]{0:T(1024)}, u32[]{:S(2)}) copy-start(f32[2048]{0:T(1024)} %copy-done.6) | copy-start | bytes 24580
Sparse Core Ops, SparseCore 0:
  13.6 88.8 all-gather.3
  326.0 199.0 reduce-scatter.1
where the time goes:
time: 565 us; the launch traced here: 564 us
  matrix products  238 us (42%)
  waiting for transfers between devices  188 us (33%)
  blocking collectives  68.4 us (12%)
  other arithmetic  54.8 us (10%)
  between operations  14.2 us (3%)
    reduce_scatter x1, waiting for transfers between devices, local_step(): d_normed = lax.psum_scatter(d_part, 'vp', scatter_dimension=0, tiled=True)  120 us
    dot_general x1, matrix products, local_step(): logits = jnp.dot(normed_all, w_local, preferred_element_type=jnp.float32)  80 us
    dot_general x1, matrix products, local_step(): lax.dot_general(d_logits, w_local, (((1,), (1,)), ((), ())), preferred_el...  79.3 us
    dot_general x1, matrix products, local_step(): lax.dot_general(normed_all, d_logits, (((0,), (0,)), ((), ())), preferred...  79.2 us
    all_gather x1, waiting for transfers between devices, local_step(): normed_all = lax.all_gather(normed, 'vp', axis=0, tiled=True)  67.6 us
    psum x1, blocking collectives, local_step(): target = lax.psum(jnp.sum(jnp.where(is_target, logits, 0.0), axis=1), 'vp')  23.4 us
    convert_element_type x1, other arithmetic, local_step(): ((prob_all - jnp.where(is_target, 1.0, 0.0)) * tok_scale[:, None]).astype...  22 us
    reduce_sum x1, other arithmetic, local_step(): sum_exp = lax.psum(jnp.sum(shifted, axis=1), 'vp')  16.5 us
  transfers between devices with their start and end apart: 2, of which 2 were waited for; matrix products, arithmetic and copies ran while one was open for 14% of the time, Pallas kernels for 0%

commit v1 on v0

v1 whole, which is shorter than its diff:
```python
import functools

import jax
import jax.numpy as jnp
from jax import lax
from jax.experimental import pallas as pl
from jax.experimental.pallas import tpu as pltpu
from jax.sharding import PartitionSpec as P


NORM_EPS = 1e-5
PAD_COLS = 128
BLK = 512
F32 = jnp.float32
BF16 = jnp.bfloat16


ANY = pl.BlockSpec(memory_space=pl.ANY)


def whole(shape):
    return pl.BlockSpec(shape, lambda *_: (0,) * len(shape))


def params(n_axes):
    return pltpu.CompilerParams(
        dimension_semantics=("arbitrary",) * n_axes, vmem_limit_bytes=60 * 1024 * 1024)


LOWEST = -3.4028234663852886e38


def fwd_body(k, n_parts, blk, limit_ref, wt_ref, *refs):
    a_refs = refs[:n_parts]
    z_ref, stat_ref, hold_ref = refs[-3:]
    step, steps = pl.program_id(0), pl.num_programs(0)
    pairs = [a_refs[i:i + 2] for i in range(0, n_parts, 2)]
    wide = 2 * a_refs[0].shape[0]

    def dots():
        for i, (lo, hi) in enumerate(pairs):
            a = jnp.concatenate([lo[...], hi[...]], axis=0)
            hold_ref[:, i * wide:(i + 1) * wide] = lax.dot_general(
                wt_ref[...], a, (((1,), (1,)), ((), ())), preferred_element_type=F32)

    def finish():
        for i in range(len(pairs)):
            cols = slice(i * wide, (i + 1) * wide)
            z = hold_ref[:, cols]
            col = (step - 1) * blk + lax.broadcasted_iota(jnp.int32, z.shape, 0)
            z = jnp.where(col < limit_ref[0], z, -jnp.inf)
            z_ref[:, cols] = z
            old = stat_ref[k:k + 1, cols]
            new = jnp.maximum(old, jnp.max(z, axis=0, keepdims=True))
            total = jnp.sum(jnp.exp(z - new), axis=0, keepdims=True)
            stat_ref[k:k + 1, cols] = new
            stat_ref[4 + k:5 + k, cols] = stat_ref[4 + k:5 + k, cols] * jnp.exp(old - new) + total

    @pl.when(step == 0)
    def _():
        stat_ref[...] = jnp.zeros(stat_ref.shape, F32) if k == 0 else refs[n_parts][...]
        stat_ref[k:k + 1, :] = jnp.full((1, stat_ref.shape[1]), LOWEST, F32)
        stat_ref[4 + k:5 + k, :] = jnp.zeros((1, stat_ref.shape[1]), F32)
        dots()

    @pl.when((step > 0) & (step < steps - 1))
    def _():
        finish()
        dots()

    pl.when(step == steps - 1)(finish)


def fwd_call(k, parts, wt, limit, stats):
    vocab, dim = wt.shape
    toks = sum(p.shape[0] for p in parts)
    blocks = pl.cdiv(vocab, BLK)
    return pl.pallas_call(
        functools.partial(fwd_body, k, len(parts), BLK),
        grid=(blocks + 1,),
        in_specs=[pl.BlockSpec(memory_space=pltpu.SMEM), pl.BlockSpec((BLK, dim), lambda j: (jnp.minimum(j, blocks - 1), 0))]
        + [whole(p.shape) for p in parts] + [whole((8, toks))] * len(stats),
        out_specs=[pl.BlockSpec((BLK, toks), lambda j: (jnp.maximum(j - 1, 0), 0)), whole((8, toks))],
        out_shape=[jax.ShapeDtypeStruct((vocab, toks), F32), jax.ShapeDtypeStruct((8, toks), F32)],
        scratch_shapes=[pltpu.VMEM((BLK, toks), F32)],
        compiler_params=params(1),
        cost_estimate=pl.CostEstimate(
            flops=2 * vocab * dim * toks, bytes_accessed=vocab * dim * 2 + vocab * toks * 4,
            transcendentals=vocab * toks),
        name="fwd",
    )(limit, wt, *parts, *stats)


TILE = 1024


def mix(first, keep_ref, got_ref, outs):
    q = keep_ref[...] + got_ref[...]
    dhalf = q.shape[1] // 2

    @pl.when(first)
    def _():
        outs[0][...], outs[1][...] = q[:, :dhalf], q[:, dhalf:]

    @pl.when(jnp.logical_not(first))
    def _():
        outs[2][...], outs[3][...] = q[:, :dhalf], q[:, dhalf:]


def back_body(k, mixing, blk, vocab, label_ref, lse_ref, scale_ref, loss_ref, z_ref, wt_ref, *refs):
    dz_ref, keep_ref, send_ref, lost_ref = refs[-10:-6] if mixing else refs[-6:-2]
    acc_ref, sem = refs[-2:]
    step, steps = pl.program_id(0), pl.num_programs(0)
    tail = vocab - (vocab // blk) * blk or blk
    rows, dim = keep_ref.shape
    row = slice(k, k + 1)

    @pl.when(step == 0)
    def _():
        acc_ref[...] = jnp.zeros_like(acc_ref)
        lost_ref[...] = loss_ref[...]

    if mixing:
        mix(step < steps // 2, refs[0], refs[1], refs[-6:-2])

    def run(size, leave):
        z = z_ref[:size]
        col = step * blk + lax.broadcasted_iota(jnp.int32, z.shape, 0)
        hit = col == label_ref[row]
        scale = scale_ref[row]
        dz = ((jnp.exp(z - lse_ref[row]) - jnp.where(hit, 1.0, 0.0)) * scale).astype(BF16)
        dz_ref[:size] = dz
        lost = jnp.sum(jnp.where(hit, z, 0.0), axis=0, keepdims=True) * scale
        wide = lost_ref.shape[1]
        lost_ref[0:1] = lost_ref[0:1] - sum(lost[:, i:i + wide] for i in range(0, lost.shape[1], wide))
        copies = []
        for t in range(dim // TILE):
            cols = slice(t * TILE, (t + 1) * TILE)
            acc_ref[:, cols] += lax.dot_general(
                dz, wt_ref[:size, cols], (((0,), (0,)), ((), ())), preferred_element_type=F32)
            if leave:
                for h, out in enumerate((keep_ref, send_ref)):
                    copies.append(pltpu.make_async_copy(
                        acc_ref.at[h * rows:(h + 1) * rows, cols], out.at[:, cols], sem.at[2 * t + h]))
                    copies[-1].start()
        for c in copies:
            c.wait()

    pl.when(step < steps - 1)(lambda: run(blk, False))
    pl.when(step == steps - 1)(lambda: run(tail, True))


def back_call(k, z, wt, label, lse, scale, loss, shared, pair):
    vocab, dim = wt.shape
    toks = z.shape[1]
    rows = toks // 2
    steps = pl.cdiv(vocab, BLK)
    mixing = bool(pair)
    in_specs = [whole((8, toks))] * 3 + [whole((8, 128)), pl.BlockSpec((BLK, toks), lambda j: (j, 0)),
                                         pl.BlockSpec((BLK, dim), lambda j: (j, 0))]
    out_specs = [pl.BlockSpec((BLK, toks), lambda j: (j, k)), ANY, ANY, whole((8, 128))]
    out_shape = [jax.ShapeDtypeStruct((vocab, 4 * toks), BF16), jax.ShapeDtypeStruct((rows, dim), F32),
                 jax.ShapeDtypeStruct((rows, dim), F32), jax.ShapeDtypeStruct((8, 128), F32)]
    if mixing:
        blk, mid, dhalf = rows // steps, steps // 2, dim // 2
        low = pl.BlockSpec((blk, dhalf), lambda j: (jnp.minimum(j, mid - 1), 0))
        high = pl.BlockSpec((blk, dhalf), lambda j: (jnp.maximum(j - mid, 0), 0))
        in_specs += [pl.BlockSpec((blk, dim), lambda j: (j, 0))] * 2
        out_specs += [low, low, high, high]
        out_shape += [jax.ShapeDtypeStruct((rows // 2, dhalf), F32)] * 4
    args = [label, lse, scale, loss, z, wt, *pair, *shared]
    return pl.pallas_call(
        functools.partial(back_body, k, mixing, BLK, vocab),
        grid=(steps,),
        in_specs=in_specs + [ANY] * len(shared),
        out_specs=out_specs,
        out_shape=out_shape,
        input_output_aliases={len(args) - 1: 0} if shared else {},
        scratch_shapes=[pltpu.VMEM((toks, dim), F32), pltpu.SemaphoreType.DMA((2 * dim // TILE,))],
        compiler_params=params(1),
        cost_estimate=pl.CostEstimate(
            flops=2 * vocab * dim * toks, bytes_accessed=vocab * dim * 2 + vocab * toks * 6,
            transcendentals=vocab * toks),
        name="back",
    )(*args)


def weight_body(n_parts, dz_ref, *refs):
    a_refs, out_ref, tick_ref = refs[:n_parts], refs[-2], refs[-1]
    tick_ref[...] = jnp.zeros_like(tick_ref)

    @pl.loop(0, out_ref.shape[1] // TILE)
    def _(k):
        cols = pl.ds(pl.multiple_of(k * TILE, TILE), TILE)
        a = jnp.concatenate([r[:, cols] for r in a_refs], axis=0)
        out_ref[:, cols] = jnp.dot(dz_ref[...], a, preferred_element_type=F32)


def weight_call(dz, parts):
    vocab, toks = dz.shape
    dim = parts[0].shape[1]
    rows, cols = 1024, dim // 2
    return pl.pallas_call(
        functools.partial(weight_body, len(parts)),
        grid=(dim // cols, pl.cdiv(vocab, rows)),
        in_specs=[pl.BlockSpec((rows, toks), lambda n, j: (j, 0))]
        + [pl.BlockSpec((p.shape[0], cols), lambda n, j: (0, n)) for p in parts],
        out_specs=[pl.BlockSpec((rows, cols), lambda n, j: (j, n)), whole((8, 128))],
        out_shape=[jax.ShapeDtypeStruct((vocab, dim), F32), jax.ShapeDtypeStruct((8, 128), F32)],
        compiler_params=params(2),
        cost_estimate=pl.CostEstimate(
            flops=2 * vocab * dim * toks, bytes_accessed=vocab * dim * 4 + vocab * toks * 4, transcendentals=0),
        name="dweight",
    )(dz, *parts)


def norm_body(hid_ref, gain_ref, lo_ref, hi_ref):
    step = pl.program_id(0)
    x = hid_ref[...].astype(F32)
    inv = lax.rsqrt(jnp.mean(x * x, axis=-1, keepdims=True) + NORM_EPS)
    a = (x * inv * gain_ref[...]).astype(BF16)

    @pl.when(step < pl.num_programs(0) // 2)
    def _():
        lo_ref[...] = a

    @pl.when(step >= pl.num_programs(0) // 2)
    def _():
        hi_ref[...] = a


def norm_call(hidden, gain, order):
    rows, dim = hidden.shape
    steps = 2
    blk, mid = rows // steps, steps // 2
    body = lambda *refs: norm_body(refs[0], refs[1], refs[-2], refs[-1])
    return pl.pallas_call(
        body,
        grid=(steps,),
        in_specs=[pl.BlockSpec((blk, dim), lambda i: (i, 0)), whole((1, dim))] + [ANY] * len(order),
        out_specs=[pl.BlockSpec((blk, dim), lambda i: (jnp.minimum(i, mid - 1), 0)),
                   pl.BlockSpec((blk, dim), lambda i: (jnp.maximum(i - mid, 0), 0))],
        out_shape=[jax.ShapeDtypeStruct((rows // 2, dim), BF16)] * 2,
        compiler_params=params(1),
        cost_estimate=pl.CostEstimate(flops=5 * rows * dim, bytes_accessed=rows * dim * 4, transcendentals=rows),
        name="norm",
    )(hidden, gain[None], *order)


def peer(me, mask):
    out = me
    for bit in (1, 2, 4):
        if mask & bit:
            out = out + bit * (1 - 2 * ((me // bit) % 2))
    return out


def push_all(n, sends, send_sem, recv_sem):
    me = lax.axis_index("vp")
    barrier = pltpu.get_barrier_semaphore()
    for m in range(1, n):
        pl.semaphore_signal(barrier, inc=1, device_id={"vp": peer(me, m)}, device_id_type=pl.DeviceIdType.MESH)
    pl.semaphore_wait(barrier, n - 1)
    copies = [
        pltpu.make_async_remote_copy(
            src_ref=src, dst_ref=got.at[m], send_sem=send_sem.at[i, m], recv_sem=recv_sem.at[i, m],
            device_id={"vp": peer(me, m)}, device_id_type=pl.DeviceIdType.MESH)
        for m in range(1, n) for i, (src, got) in enumerate(sends)
    ]
    for c in copies:
        c.start()
    for c in copies:
        c.wait()


def tree(v):
    while len(v) > 1:
        v = [v[i] + v[i + 1] for i in range(0, len(v), 2)]
    return v[0]


def sum_body(n, gain_ref, loss_ref, gain_out, loss_out, got_gain, got_loss, send_sem, recv_sem):
    push_all(n, [(gain_ref, got_gain), (loss_ref, got_loss)], send_sem, recv_sem)
    gain_out[...] = tree([gain_ref[...]] + [got_gain[m] for m in range(1, n)])
    loss_out[...] = tree([loss_ref[...]] + [got_loss[m] for m in range(1, n)])


LAYOUT = (
    ((0, 0), (0, 1), (1, 0), (1, 1)),
    ((2, 0), (4, 0), (3, 0), (5, 0)),
    ((2, 1), (4, 1), (3, 1), (5, 1)),
    ((6, 0), (6, 1), (7, 0), (7, 1)),
)


def stats_body(n, vocab, stat_ref, label_ref, weight_ref, label_out, lse_out, scale_out, loss_out,
               got_stat, got_label, got_weight, send_sem, recv_sem):
    push_all(n, [(stat_ref, got_stat), (label_ref, got_label), (weight_ref, got_weight)], send_sem, recv_sem)
    width = stat_ref.shape[1] // 4
    base = lax.axis_index("vp") * vocab
    place = {key: (k, i) for k, row in enumerate(LAYOUT) for i, key in enumerate(row)}
    pick = lambda own, got, m, *at: own[at] if m == 0 else got[(m,) + at]
    lanes = lambda i: slice(i * width, (i + 1) * width)
    one = lambda k: slice(k, k + 1)
    total_weight = tree([
        jnp.sum(pick(weight_ref, got_weight, m, slice(0, 2)), axis=(0, 1), keepdims=True) for m in range(n)])
    loss = jnp.zeros((1, width), F32)
    label_out[4:] = jnp.zeros((4, 4 * width), jnp.int32)
    lse_out[4:] = jnp.zeros((4, 4 * width), F32)
    scale_out[4:] = jnp.zeros((4, 4 * width), F32)
    for k, row in enumerate(LAYOUT):
        for i, (r, h) in enumerate(row):
            tops, sums = [], []
            for m in range(n):
                kk, ii = place[(r ^ m, h)]
                tops.append(pick(stat_ref, got_stat, m, one(kk), lanes(ii)))
                sums.append(pick(stat_ref, got_stat, m, one(4 + kk), lanes(ii)))
            top = functools.reduce(jnp.maximum, tops)
            lse = top + jnp.log(tree([s * jnp.exp(t - top) for s, t in zip(sums, tops)]))
            scale = pick(weight_ref, got_weight, r, one(h)) / total_weight
            lse_out[one(k), lanes(i)] = lse
            scale_out[one(k), lanes(i)] = scale
            label_out[one(k), lanes(i)] = pick(label_ref, got_label, r, one(h)) - base
            if r == 0:
                loss = loss + scale * lse
    loss_out[...] = jnp.zeros(loss_out.shape, F32)
    loss_out[0:1] = loss


def small_call(body, n, args, outs, ident):
    vm = pl.BlockSpec(memory_space=pltpu.VMEM)
    sems = [pltpu.SemaphoreType.DMA((len(args), n))] * 2
    return pl.pallas_call(
        body,
        in_specs=[vm] * len(args),
        out_specs=[vm] * len(outs),
        out_shape=outs,
        scratch_shapes=[pltpu.VMEM((n,) + v.shape, v.dtype) for v in args] + sems,
        compiler_params=pltpu.CompilerParams(collective_id=ident, has_side_effects=True),
        cost_estimate=pl.CostEstimate(flops=4000, bytes_accessed=4_000_000, transcendentals=0),
    )(*args)


def mix_body(keep_ref, got_ref, a_ref, b_ref):
    q = keep_ref[...] + got_ref[...]
    dhalf = q.shape[1] // 2
    a_ref[...], b_ref[...] = q[:, :dhalf], q[:, dhalf:]


def mix_call(keep, got):
    rows, dim = keep.shape
    steps = 4
    blk, dhalf = rows // steps, dim // 2
    full = pl.BlockSpec((blk, dim), lambda i: (i, 0))
    return pl.pallas_call(
        mix_body,
        grid=(steps,),
        in_specs=[full, full],
        out_specs=[pl.BlockSpec((blk, dhalf), lambda i: (i, 0))] * 2,
        out_shape=[jax.ShapeDtypeStruct((rows, dhalf), F32)] * 2,
        compiler_params=params(1),
        cost_estimate=pl.CostEstimate(flops=rows * dim, bytes_accessed=rows * dim * 12, transcendentals=0),
        name="mix",
    )(keep, got)


def second_body(keep2_ref, keep4_ref, got2_ref, got4_ref, sa_ref, ta_ref, xa_ref, xb_ref, ya_ref, yb_ref,
                x2_ref, y4_ref, s_ref, t_ref):
    dhalf = sa_ref.shape[1]
    q2 = keep2_ref[...] + got2_ref[...]
    q4 = keep4_ref[...] + got4_ref[...]
    x2_ref[...] = q2[:, :dhalf]
    y4_ref[...] = q4[:, dhalf:]
    s_ref[0] = sa_ref[...] + xa_ref[...]
    s_ref[1] = q4[:, :dhalf] + xb_ref[...]
    t_ref[0] = ta_ref[...] + ya_ref[...]
    t_ref[1] = q2[:, dhalf:] + yb_ref[...]


def second_call(keep, got, sa, ta, x, y):
    half, dhalf = sa.shape
    steps = 4
    blk = half // steps
    at = lambda width, off: pl.BlockSpec((blk, width), lambda i: (i + off, 0))
    two = pl.BlockSpec((2, blk, dhalf), lambda i: (0, i, 0))
    return pl.pallas_call(
        second_body,
        grid=(steps,),
        in_specs=[at(2 * dhalf, 0), at(2 * dhalf, steps), at(2 * dhalf, 0), at(2 * dhalf, steps), at(dhalf, 0), at(dhalf, 0),
                  at(dhalf, 0), at(dhalf, steps), at(dhalf, 0), at(dhalf, steps)],
        out_specs=[at(dhalf, 0), at(dhalf, 0), two, two],
        out_shape=[jax.ShapeDtypeStruct((half, dhalf), F32)] * 2 + [jax.ShapeDtypeStruct((2, half, dhalf), F32)] * 2,
        compiler_params=params(1),
        cost_estimate=pl.CostEstimate(flops=8 * half * dhalf, bytes_accessed=half * dhalf * 80, transcendentals=0),
        name="second",
    )(keep, keep, got, got, sa, ta, x, x, y, y)


def last_body(hid_ref, gain_ref, keep_ref, got_ref, x2a_ref, x2b_ref, s4_ref, y4a_ref, y4b_ref, t2_ref, tick_ref,
              dh_ref, dgain_ref):
    del tick_ref
    step = pl.program_id(0)
    dhalf = s4_ref.shape[1]

    def run(x2_ref, y4_ref):
        q = keep_ref[...] + got_ref[...]
        g = jnp.concatenate(
            [q[:, :dhalf] + x2_ref[...] + s4_ref[...], q[:, dhalf:] + y4_ref[...] + t2_ref[...]], axis=1)
        x = hid_ref[...].astype(F32)
        inv = lax.rsqrt(jnp.mean(x * x, axis=-1, keepdims=True) + NORM_EPS)
        norm = x * inv
        u = g * gain_ref[...]
        dh_ref[...] = (inv * (u - norm * jnp.mean(u * norm, axis=-1, keepdims=True))).astype(BF16)
        part = jnp.sum(g * norm, axis=0, keepdims=True)
        wide = dgain_ref.shape[1]
        for k in range(dgain_ref.shape[0]):
            piece = part[:, k * wide:(k + 1) * wide]
            dgain_ref[k:k + 1] = jnp.where(step == 0, piece, dgain_ref[k:k + 1] + piece)

    pl.when(step < pl.num_programs(0) // 2)(lambda: run(x2a_ref, y4a_ref))
    pl.when(step >= pl.num_programs(0) // 2)(lambda: run(x2b_ref, y4b_ref))


def last_call(hidden, gain, keep, got, x2a, x2b, s4, y4a, y4b, t2, tick):
    rows, dim = hidden.shape
    steps = 8
    blk, mid, dhalf = rows // steps, steps // 2, dim // 2
    row = lambda width: pl.BlockSpec((blk, width), lambda i: (i, 0))
    low = pl.BlockSpec((blk, dhalf), lambda i: (jnp.minimum(i, mid - 1), 0))
    high = pl.BlockSpec((blk, dhalf), lambda i: (jnp.maximum(i - mid, 0), 0))
    return pl.pallas_call(
        last_body,
        grid=(steps,),
        in_specs=[row(dim), whole((1, dim)), row(dim), row(dim), low, high, row(dhalf), low, high, row(dhalf), ANY],
        out_specs=[row(dim), whole((8, dim // 8))],
        out_shape=[jax.ShapeDtypeStruct((rows, dim), BF16), jax.ShapeDtypeStruct((8, dim // 8), F32)],
        compiler_params=params(1),
        cost_estimate=pl.CostEstimate(flops=20 * rows * dim, bytes_accessed=rows * dim * 20, transcendentals=rows),
        name="last",
    )(hidden, gain[None], keep, got, x2a, x2b, s4, y4a, y4b, t2, tick)


def solution(mesh):
    n = mesh.shape["vp"]

    def swap(v, mask):
        return lax.ppermute(v, "vp", [(i, i ^ mask) for i in range(n)])

    def compute(hidden, labels, loss_weight, norm_gain, w_local):
        rows, dim = hidden.shape
        half, dhalf = rows // 2, dim // 2
        wt = w_local.T
        vocab_local = wt.shape[0]
        vocab_real = vocab_local * n - PAD_COLS
        me = lax.axis_index("vp")

        limit = jnp.minimum(vocab_real - me * vocab_local, vocab_local).astype(jnp.int32).reshape(1)

        r0a, r0b = norm_call(hidden, norm_gain, [])
        r2a, r4a = swap(r0a, 2), swap(r0a, 4)
        r1a, r1b = swap(r0a, 1), swap(r0b, 1)
        r2b, r4b = swap(r0b, 2), swap(r0b, 4)
        r3a, r5a = swap(r2a, 1), swap(r4a, 1)
        r3b, r5b = swap(r2b, 1), swap(r4b, 1)
        r6a, r6b = swap(r2a, 4), swap(r4b, 2)
        r7a, r7b = swap(r6a, 1), swap(r6b, 1)
        groups = [[r0a, r0b, r1a, r1b], [r2a, r4a, r3a, r5a], [r2b, r4b, r3b, r5b], [r6a, r6b, r7a, r7b]]

        logits_g, stats = [], []
        for k, parts in enumerate(groups):
            logits, stat = fwd_call(k, parts, wt, limit, stats)
            logits_g.append(logits)
            stats = [stat]

        spec = jax.ShapeDtypeStruct
        label, lse, scale, loss = small_call(
            functools.partial(stats_body, n, vocab_local), n,
            [stats[0], labels.reshape(2, half), loss_weight.reshape(2, half)],
            [spec((8, 2 * rows), jnp.int32), spec((8, 2 * rows), F32), spec((8, 2 * rows), F32), spec((8, half), F32)],
            0)

        def back(k, loss, shared, pair):
            return back_call(k, logits_g[k], wt, label, lse, scale, loss, shared, pair)

        dz, keep3, send3, loss = back(3, loss, [], [])
        got3 = swap(send3, 1)
        dz, keep1, send1, loss = back(1, loss, [dz], [])
        q6x, q6y = mix_call(keep3, got3)
        x6, y6 = swap(q6x, 2), swap(q6y, 4)
        got1 = swap(send1, 1)
        dz, keep2, send2, loss = back(2, loss, [dz], [])
        got2 = swap(send2, 1)
        dz, keep0, send0, loss, x2a, ta, sa, y4a = back(0, loss, [dz], [keep1, got1])
        x2a, y4a = swap(x2a, 2), swap(y4a, 4)
        got0 = swap(send0, 1)
        x2b, y4b, s4, t2 = second_call(keep2, got2, sa, ta, x6, y6)
        x2b, y4b = swap(x2b, 2), swap(y4b, 4)
        s4, t2 = swap(s4, 4).reshape(rows, dhalf), swap(t2, 2).reshape(rows, dhalf)

        dwt, tick = weight_call(dz, [p for g in groups for p in g])
        d_input, d_gain = last_call(hidden, norm_gain, keep0, got0, x2a, x2b, s4, y4a, y4b, t2, tick)
        d_gain, loss = small_call(
            functools.partial(sum_body, n), n, [d_gain, loss], [spec(d_gain.shape, F32), spec(loss.shape, F32)], 1)
        return jnp.sum(loss[0]).reshape(1), d_input, dwt.T, d_gain.reshape(dim)

    return jax.shard_map(
        compute,
        mesh=mesh,
        in_specs=(P(("dp", "vp"), None), P(("dp", "vp")), P(("dp", "vp")), P(None), P(None, "vp")),
        out_specs=(P("dp"), P(("dp", "vp"), None), P("dp", "vp"), P("dp")),
        check_vma=False,
    )
```

time: 565 us -> 439 us (0.78); the launches traced: 564 us -> 431 us
  Pallas kernels: 0 us -> 333 us
  matrix products: 238 us -> 0 us
  waiting for transfers between devices: 188 us -> 72.1 us
  blocking collectives: 68.4 us -> 0 us
  other arithmetic: 54.8 us -> 1.28 us
  starting transfers between devices: 0.08 us -> 19.1 us
  between operations: 14.2 us -> 1.09 us
    pallas_call x0 -> x15, Pallas kernels: none -> 333 us  [the longest x4 110 us: back_call(): pl.pallas_call(functools.partial(back_body, k, mixing, BLK, vocab), grid=...]
    dot_general x3 -> x0, matrix products: 238 us -> none  [the longest x1 80 us: local_step(): logits = jnp.dot(normed_all, w_local, preferred_element_type=jnp.float32)]
    reduce_scatter x1 -> x0, waiting for transfers between devices: 120 us -> none  [local_step(): d_normed = lax.psum_scatter(d_part, 'vp', scatter_dimension=0, tiled=True)]
    ppermute x0 -> x26, waiting for transfers between devices: none -> 72.1 us  [swap(): return lax.ppermute(v, 'vp', [(i, i ^ mask) for i in range(n)])]
    all_gather x1 -> x0, waiting for transfers between devices: 67.6 us -> none  [local_step(): normed_all = lax.all_gather(normed, 'vp', axis=0, tiled=True)]
    psum x2 -> x0, blocking collectives: 35.4 us -> none  [the longest x1 23.4 us: local_step(): target = lax.psum(jnp.sum(jnp.where(is_target, logits, 0.0), axis=1), 'vp')]
    convert_element_type x3 -> x0, other arithmetic: 30.2 us -> none  [the longest x1 22 us: local_step(): ((prob_all - jnp.where(is_target, 1.0, 0.0)) * tok_scale[:, None]).astype...]
    reduce_sum x5 -> x1, other arithmetic: 23.3 us -> 1.28 us  [compute(): return (jnp.sum(loss[0]).reshape(1), d_input, dwt.T, d_gain.reshape(dim))]
  transfers between devices with their start and end apart: 2 -> 26, of which waited for: 2 -> 7; matrix products, arithmetic and copies ran while one was open for 14% -> 0% of each run, Pallas kernels for 0% -> 58%
where the time goes in v1:
time: 439 us; the launch traced here: 431 us
  Pallas kernels  333 us (76%)
  waiting for transfers between devices  72.1 us (16%)
  starting transfers between devices  19.1 us (4%)
    pallas_call x4, Pallas kernels, back_call(): pl.pallas_call(functools.partial(back_body, k, mixing, BLK, vocab), grid=...  110 us
    pallas_call x4, Pallas kernels, fwd_call(): pl.pallas_call(functools.partial(fwd_body, k, len(parts), BLK), grid=(blo...  99 us
    pallas_call x1, Pallas kernels, weight_call(): pl.pallas_call(functools.partial(weight_body, len(parts)), grid=(dim // c...  80.5 us
    ppermute x26, waiting for transfers between devices, swap(): return lax.ppermute(v, 'vp', [(i, i ^ mask) for i in range(n)])  72.1 us
    ppermute x26, starting transfers between devices, swap(): return lax.ppermute(v, 'vp', [(i, i ^ mask) for i in range(n)])  19.1 us
    pallas_call x2, Pallas kernels, small_call(): pl.pallas_call(body, in_specs=[vm] * len(args), out_specs=[vm] * len(outs...  14.8 us
    pallas_call x1, Pallas kernels, last_call(): pl.pallas_call(last_body, grid=(steps,), in_specs=[row(dim), whole((1, di...  11 us
  transfers between devices with their start and end apart: 26, of which 7 were waited for; matrix products, arithmetic and copies ran while one was open for 0% of the time, Pallas kernels for 58%

profile of v1, /device:TPU:0, one launch (start us, length us, event | category | flops | bytes accessed | tf_op | source)
XLA Modules:
  0.0 430.7 jit_solution(2408691705979229821)
XLA Ops:
  0.6 3.8 norm.1
  5.2 2.5 collective-permute-start
  7.6 1.5 collective-permute-start.9
  10.5 21.3 %collective-permute-done.refs_0_.refs_4_ = bf16[128,4096]{1,0:T(8,128)(2,1)S(1)} collective-permute-done((bf16[128,4096]{1,0:T(8,128)(2,1)}, bf16[128,4096]{1,0:T(8,128)(2,1)S(1)}, u32[]{:S(2)}, u32[]{:S(2)}) %collective-permute-start) | collective-permute-done | bytes 1048608 | tf_op jit(solution)/shard_map/ppermute | solution.py:447
  31.9 2.0 collective-permute-done.9.refs_1_.refs_5_
  33.9 1.5 collective-permute-start.1
  35.4 21.0 %collective-permute-done.2.refs_1_.refs_9_ = bf16[128,4096]{1,0:T(8,128)(2,1)} collective-permute-done((bf16[128,4096]{1,0:T(8,128)(2,1)}, bf16[128,4096]{1,0:T(8,128)(2,1)}, u32[]{:S(2)}, u32[]{:S(2)}) %collective-permute-start.2) | collective-permute-done | bytes 1048608 | tf_op jit(solution)/shard_map/ppermute | solution.py:447
  56.5 24.6 %fwd.4 = (f32[4016,512]{1,0:T(8,128)}, f32[8,512]{1,0:T(8,128)}) custom-call(s32[1]{0:T(128)} %bitcast.1.limit_ref, bf16[4016,4096]{1,0:T(8,128)(2,1)} %bitcast.11, bf16[128,4096]{1,0:T(8,128)(2,1)} %get-tuple-element.50.refs_0_, bf16[128,4096]{1,0:T(8,128)(2,1)} %get-tuple-element.51.refs_1_, bf16[128,4096]{1,0:T(8,128)(2,1)} %copy-done.3, ...), custom_call_target="tpu_custom_call" | custom-call | flops 16844324864 | bytes 41123840 | tf_op jit(solution)/shard_map/fwd/pallas_call | solution.py:78
  82.2 24.6 %fwd.5 = (f32[4016,512]{1,0:T(8,128)}, f32[8,512]{1,0:T(8,128)}) custom-call(s32[1]{0:T(128)} %bitcast.1.limit_ref, bf16[4016,4096]{1,0:T(8,128)(2,1)} %bitcast.12, bf16[128,4096]{1,0:T(8,128)(2,1)} %copy-done.4, bf16[128,4096]{1,0:T(8,128)(2,1)} %copy-done.5, bf16[128,4096]{1,0:T(8,128)(2,1)} %collective-permute-done.10.refs_2_.refs_6_, ...), custom_call_target="tpu_custom_call" | custom-call | flops 16844324864 | bytes 41123840 | tf_op jit(solution)/shard_map/fwd/pallas_call | solution.py:78
  108.2 25.2 %fwd.6 = (f32[4016,512]{1,0:T(8,128)}, f32[8,512]{1,0:T(8,128)}) custom-call(s32[1]{0:T(128)} %bitcast.1.limit_ref, bf16[4016,4096]{1,0:T(8,128)(2,1)} %bitcast.13, bf16[128,4096]{1,0:T(8,128)(2,1)} %collective-permute-done.6.refs_0_.refs_8_, bf16[128,4096]{1,0:T(8,128)(2,1)} %collective-permute-done.2.refs_1_.refs_9_, bf16[128,4096]{1,0:T(8,128)(2,1)} %copy-done.7, ...), custom_call_target="tpu_custom_call" | custom-call | flops 16844324864 | bytes 41123840 | tf_op jit(solution)/shard_map/fwd/pallas_call | solution.py:78
  133.4 24.6 %fwd.7 = (f32[4016,512]{1,0:T(8,128)}, f32[8,512]{1,0:T(8,128)}) custom-call(s32[1]{0:T(128)} %bitcast.1.limit_ref, bf16[4016,4096]{1,0:T(8,128)(2,1)} %bitcast.14, bf16[128,4096]{1,0:T(8,128)(2,1)} %collective-permute-done.1.refs_0_.refs_12_, bf16[128,4096]{1,0:T(8,128)(2,1)} %collective-permute-done.3.refs_1_.refs_13_, ...), custom_call_target="tpu_custom_call" | custom-call | flops 16844324864 | bytes 41123840 | tf_op jit(solution)/shard_map/fwd/pallas_call | solution.py:78
  158.0 7.8 %shard_map.84 = (s32[8,512]{1,0:T(8,128)}, f32[8,512]{1,0:T(8,128)}, f32[8,512]{1,0:T(8,128)}, f32[8,128]{1,0:T(8,128)}) custom-call(f32[8,512]{1,0:T(8,128)} %get-tuple-element.55.stat_ref, s32[2,128]{1,0:T(2,128)} %bitcast.24, f32[2,128]{1,0:T(2,128)} %bitcast.25), custom_call_target="tpu_custom_call" | custom-call | flops 4000 | bytes 4000000 | tf_op jit(solution)/shard_map/pallas_call | solution.py:333
  165.8 27.1 %back.4 = (bf16[4016,2048]{1,0:T(8,128)(2,1)}, f32[256,4096]{1,0:T(8,128)}, f32[256,4096]{1,0:T(8,128)}, f32[8,128]{1,0:T(8,128)}) custom-call(s32[8,512]{1,0:T(8,128)} %get-tuple-element.56.label_ref, f32[8,512]{1,0:T(8,128)} %get-tuple-element.57.lse_ref, f32[8,512]{1,0:T(8,128)} %get-tuple-element.58.scale_ref, f32[8,128]{1,0:T(8,128)} %get-tuple-element.59.loss_ref, ...), custom_call_target="tpu_custom_call" | custom-call | flops 16844324864 | bytes 45236224 | tf_op jit(solution)/shard_map/back/pallas_call | solution.py:172
  193.0 27.2 %back.5 = (bf16[4016,2048]{1,0:T(8,128)(2,1)}, f32[256,4096]{1,0:T(8,128)}, f32[256,4096]{1,0:T(8,128)}, f32[8,128]{1,0:T(8,128)}) custom-call(s32[8,512]{1,0:T(8,128)} %get-tuple-element.56.label_ref, f32[8,512]{1,0:T(8,128)} %get-tuple-element.57.lse_ref, f32[8,512]{1,0:T(8,128)} %get-tuple-element.58.scale_ref, ...), custom_call_target="tpu_custom_call", output_to_operand_aliasing={{0}: (6, {})} | custom-call | flops 16844324864 | bytes 45236224 | tf_op jit(solution)/shard_map/back/pallas_call | solution.py:172
  220.7 27.1 %back.6 = (bf16[4016,2048]{1,0:T(8,128)(2,1)}, f32[256,4096]{1,0:T(8,128)}, f32[256,4096]{1,0:T(8,128)}, f32[8,128]{1,0:T(8,128)}) custom-call(s32[8,512]{1,0:T(8,128)} %get-tuple-element.56.label_ref, f32[8,512]{1,0:T(8,128)} %get-tuple-element.57.lse_ref, f32[8,512]{1,0:T(8,128)} %get-tuple-element.58.scale_ref, ...), custom_call_target="tpu_custom_call", output_to_operand_aliasing={{0}: (6, {})} | custom-call | flops 16844324864 | bytes 45236224 | tf_op jit(solution)/shard_map/back/pallas_call | solution.py:172
  247.9 5.8 %mix.1 = (f32[256,2048]{1,0:T(8,128)}, f32[256,2048]{1,0:T(8,128)}) custom-call(f32[256,4096]{1,0:T(8,128)} %get-tuple-element.79.keep_ref, f32[256,4096]{1,0:T(8,128)} %collective-permute-done.18.got_ref), custom_call_target="tpu_custom_call" | custom-call | flops 1048576 | bytes 12582912 | tf_op jit(solution)/shard_map/mix/pallas_call | solution.py:355
  256.6 29.0 %back.7 = (bf16[4016,2048]{1,0:T(8,128)(2,1)}, f32[256,4096]{1,0:T(8,128)}, f32[256,4096]{1,0:T(8,128)}, f32[8,128]{1,0:T(8,128)}, f32[128,2048]{1,0:T(8,128)}, ...) custom-call(s32[8,512]{1,0:T(8,128)} %get-tuple-element.56.label_ref, ...), custom_call_target="tpu_custom_call", output_to_operand_aliasing={{0}: (8, {})} | custom-call | flops 16844324864 | bytes 45236224 | tf_op jit(solution)/shard_map/back/pallas_call | solution.py:172
  286.8 15.6 %collective-permute-done.19.xa_ref.xb_ref = f32[256,2048]{1,0:T(8,128)S(1)} collective-permute-done((f32[256,2048]{1,0:T(8,128)}, f32[256,2048]{1,0:T(8,128)S(1)}, u32[]{:S(2)}, u32[]{:S(2)}) %collective-permute-start.19) | collective-permute-done | bytes 2097184 | tf_op jit(solution)/shard_map/ppermute | solution.py:447
  302.4 1.6 collective-permute-done.20.ya_ref.yb_ref
  304.0 7.8 %second.1 = (f32[128,2048]{1,0:T(8,128)}, f32[128,2048]{1,0:T(8,128)}, f32[2,128,2048]{2,1,0:T(8,128)}, f32[2,128,2048]{2,1,0:T(8,128)}) custom-call(f32[256,4096]{1,0:T(8,128)} %get-tuple-element.75.keep2_ref.keep4_ref, f32[256,4096]{1,0:T(8,128)} %get-tuple-element.75.keep2_ref.keep4_ref, f32[256,4096]{1,0:T(8,128)} %collective-permute-done.17.got2_ref.got4_ref, ...), custom_call_target="tpu_custom_call" | custom-call | flops 2097152 | bytes 20971520 | tf_op jit(solution)/shard_map/second/pallas_call | solution.py:386
  314.5 10.3 %collective-permute-done.16.x2a_ref = f32[128,2048]{1,0:T(8,128)S(1)} collective-permute-done((f32[128,2048]{1,0:T(8,128)}, f32[128,2048]{1,0:T(8,128)S(1)}, u32[]{:S(2)}, u32[]{:S(2)}) %collective-permute-start.16) | collective-permute-done | bytes 1048608 | tf_op jit(solution)/shard_map/ppermute | solution.py:447
  327.8 80.5 %dweight.1 = (f32[4016,4096]{1,0:T(8,128)}, f32[8,128]{1,0:T(8,128)}) custom-call(bf16[4016,2048]{1,0:T(8,128)(2,1)} %get-tuple-element.88.dz_ref, bf16[128,4096]{1,0:T(8,128)(2,1)} %get-tuple-element.50.refs_0_, bf16[128,4096]{1,0:T(8,128)(2,1)} %get-tuple-element.51.refs_1_, bf16[128,4096]{1,0:T(8,128)(2,1)} %copy-done.3, ...), custom_call_target="tpu_custom_call" | custom-call | flops 67377299456 | bytes 98697216 | tf_op jit(solution)/shard_map/dweight/pallas_call | solution.py:203
  409.8 11.0 %last.1 = (bf16[256,4096]{1,0:T(8,128)(2,1)}, f32[8,512]{1,0:T(8,128)}) custom-call(bf16[256,4096]{1,0:T(8,128)(2,1)} %hid_ref.1, f32[1,4096]{1,0:T(1,128)} %bitcast.21, f32[256,4096]{1,0:T(8,128)} %get-tuple-element.72.keep_ref, f32[256,4096]{1,0:T(8,128)} %collective-permute-done.15.got_ref, f32[128,2048]{1,0:T(8,128)} %copy-done.2, ...), custom_call_target="tpu_custom_call" | custom-call | flops 20971520 | bytes 20971520 | tf_op jit(solution)/shard_map/last/pallas_call | solution.py:431
  420.8 7.0 %shard_map.85 = (f32[8,512]{1,0:T(8,128)}, f32[8,128]{1,0:T(8,128)}) custom-call(f32[8,512]{1,0:T(8,128)} %get-tuple-element.90.gain_ref, f32[8,128]{1,0:T(8,128)} %get-tuple-element.91.loss_ref), custom_call_target="tpu_custom_call" | custom-call | flops 4000 | bytes 4000000 | tf_op jit(solution)/shard_map/pallas_call | solution.py:333
  (61 shorter events, 19.1 us)
Async XLA Ops:
  5.2 26.7 %collective-permute-start = (bf16[128,4096]{1,0:T(8,128)(2,1)}, bf16[128,4096]{1,0:T(8,128)(2,1)S(1)}, u32[]{:S(2)}, u32[]{:S(2)}) collective-permute-start(bf16[128,4096]{1,0:T(8,128)(2,1)} %get-tuple-element.50.refs_0_), channel_id=1, source_target_pairs={{0,2},{1,3},{2,0},{3,1},{4,6},{5,7},{6,4},{7,5},{8,10},{9,11},{10,... | collective-permute-start | bytes 3145736 | tf_op jit(solution)/shard_map/ppermute | solution.py:447
  7.6 26.2 %collective-permute-start.9 = (bf16[128,4096]{1,0:T(8,128)(2,1)}, bf16[128,4096]{1,0:T(8,128)(2,1)S(1)}, u32[]{:S(2)}, u32[]{:S(2)}) collective-permute-start(bf16[128,4096]{1,0:T(8,128)(2,1)} %get-tuple-element.50.refs_0_), channel_id=1, source_target_pairs={{0,4},{1,5},{2,6},{3,7},{4,0},{5,1},{6,2},{7,3},{8,12},{9,13},{10,... | collective-permute-start | bytes 3145736 | tf_op jit(solution)/shard_map/ppermute | solution.py:447
  9.2 26.2 %collective-permute-start.13 = (bf16[128,4096]{1,0:T(8,128)(2,1)}, bf16[128,4096]{1,0:T(8,128)(2,1)}, u32[]{:S(2)}, u32[]{:S(2)}) collective-permute-start(bf16[128,4096]{1,0:T(8,128)(2,1)} %get-tuple-element.51.refs_1_), channel_id=1, source_target_pairs={{0,1},{1,0},{2,3},{3,2},{4,5},{5,4},{6,7},{7,6},{8,9},{9,8},{10,11... | collective-permute-start | bytes 3145736 | tf_op jit(solution)/shard_map/ppermute | solution.py:447
  9.2 47.3 %collective-permute-start.2 = (bf16[128,4096]{1,0:T(8,128)(2,1)}, bf16[128,4096]{1,0:T(8,128)(2,1)}, u32[]{:S(2)}, u32[]{:S(2)}) collective-permute-start(bf16[128,4096]{1,0:T(8,128)(2,1)} %get-tuple-element.51.refs_1_), channel_id=1, source_target_pairs={{0,4},{1,5},{2,6},{3,7},{4,0},{5,1},{6,2},{7,3},{8,12},{9,13},{10,... | collective-permute-start | bytes 3145736 | tf_op jit(solution)/shard_map/ppermute | solution.py:447
  9.7 71.4 %collective-permute-start.6 = (bf16[128,4096]{1,0:T(8,128)(2,1)}, bf16[128,4096]{1,0:T(8,128)(2,1)}, u32[]{:S(2)}, u32[]{:S(2)}) collective-permute-start(bf16[128,4096]{1,0:T(8,128)(2,1)} %get-tuple-element.51.refs_1_), channel_id=1, source_target_pairs={{0,2},{1,3},{2,0},{3,1},{4,6},{5,7},{6,4},{7,5},{8,10},{9,11},{10,... | collective-permute-start | bytes 3145736 | tf_op jit(solution)/shard_map/ppermute | solution.py:447
  31.9 50.3 %collective-permute-start.10 = (bf16[128,4096]{1,0:T(8,128)(2,1)S(1)}, bf16[128,4096]{1,0:T(8,128)(2,1)}, u32[]{:S(2)}, u32[]{:S(2)}) collective-permute-start(bf16[128,4096]{1,0:T(8,128)(2,1)S(1)} %collective-permute-done.refs_0_.refs_4_), channel_id=1, source_target_pairs={{0,1},{1,0},{2,3},{3,2},{4,5},{5,4},{6,7},{7,6},{8,9},{9,8},{10,11... | collective-permute-start | bytes 3145736 | tf_op jit(solution)/shard_map/ppermute | solution.py:447
  33.9 47.8 %collective-permute-start.1 = (bf16[128,4096]{1,0:T(8,128)(2,1)S(1)}, bf16[128,4096]{1,0:T(8,128)(2,1)}, u32[]{:S(2)}, u32[]{:S(2)}) collective-permute-start(bf16[128,4096]{1,0:T(8,128)(2,1)S(1)} %collective-permute-done.refs_0_.refs_4_), channel_id=1, source_target_pairs={{0,4},{1,5},{2,6},{3,7},{4,0},{5,1},{6,2},{7,3},{8,12},{9,13},{10,... | collective-permute-start | bytes 3145736 | tf_op jit(solution)/shard_map/ppermute | solution.py:447
  35.4 45.8 %collective-permute-start.11 = (bf16[128,4096]{1,0:T(8,128)(2,1)S(1)}, bf16[128,4096]{1,0:T(8,128)(2,1)}, u32[]{:S(2)}, u32[]{:S(2)}) collective-permute-start(bf16[128,4096]{1,0:T(8,128)(2,1)S(1)} %collective-permute-done.9.refs_1_.refs_5_), channel_id=1, source_target_pairs={{0,1},{1,0},{2,3},{3,2},{4,5},{5,4},{6,7},{7,6},{8,9},{9,8},{10,11... | collective-permute-start | bytes 3145736 | tf_op jit(solution)/shard_map/ppermute | solution.py:447
  81.1 25.7 %collective-permute-start.8 = (bf16[128,4096]{1,0:T(8,128)(2,1)}, bf16[128,4096]{1,0:T(8,128)(2,1)S(1)}, u32[]{:S(2)}, u32[]{:S(2)}) collective-permute-start(bf16[128,4096]{1,0:T(8,128)(2,1)} %collective-permute-done.2.refs_1_.refs_9_), channel_id=1, source_target_pairs={{0,1},{1,0},{2,3},{3,2},{4,5},{5,4},{6,7},{7,6},{8,9},{9,8},{10,11... | collective-permute-start | bytes 3145736 | tf_op jit(solution)/shard_map/ppermute | solution.py:447
  81.2 25.6 %collective-permute-start.7 = (bf16[128,4096]{1,0:T(8,128)(2,1)}, bf16[128,4096]{1,0:T(8,128)(2,1)S(1)}, u32[]{:S(2)}, u32[]{:S(2)}) collective-permute-start(bf16[128,4096]{1,0:T(8,128)(2,1)} %collective-permute-done.6.refs_0_.refs_8_), channel_id=1, source_target_pairs={{0,1},{1,0},{2,3},{3,2},{4,5},{5,4},{6,7},{7,6},{8,9},{9,8},{10,11... | collective-permute-start | bytes 3145736 | tf_op jit(solution)/shard_map/ppermute | solution.py:447
  81.7 51.7 %collective-permute-start.4 = (bf16[128,4096]{1,0:T(8,128)(2,1)}, bf16[128,4096]{1,0:T(8,128)(2,1)}, u32[]{:S(2)}, u32[]{:S(2)}) collective-permute-start(bf16[128,4096]{1,0:T(8,128)(2,1)} %collective-permute-done.1.refs_0_.refs_12_), channel_id=1, source_target_pairs={{0,1},{1,0},{2,3},{3,2},{4,5},{5,4},{6,7},{7,6},{8,9},{9,8},{10,11... | collective-permute-start | bytes 3145736 | tf_op jit(solution)/shard_map/ppermute | solution.py:447
  81.7 51.6 %collective-permute-start.5 = (bf16[128,4096]{1,0:T(8,128)(2,1)}, bf16[128,4096]{1,0:T(8,128)(2,1)}, u32[]{:S(2)}, u32[]{:S(2)}) collective-permute-start(bf16[128,4096]{1,0:T(8,128)(2,1)} %collective-permute-done.3.refs_1_.refs_13_), channel_id=1, source_target_pairs={{0,1},{1,0},{2,3},{3,2},{4,5},{5,4},{6,7},{7,6},{8,9},{9,8},{10,11... | collective-permute-start | bytes 3145736 | tf_op jit(solution)/shard_map/ppermute | solution.py:447
  192.9 55.0 %collective-permute-start.18 = (f32[256,4096]{1,0:T(8,128)}, f32[256,4096]{1,0:T(8,128)}, u32[]{:S(2)}, u32[]{:S(2)}) collective-permute-start(f32[256,4096]{1,0:T(8,128)} %get-tuple-element.80), channel_id=1, source_target_pairs={{0,1},{1,0},{2,3},{3,2},{4,5},{5,4},{6,7},{7,6},{8,9},{9,8},{10,11... | collective-permute-start | bytes 12582920 | tf_op jit(solution)/shard_map/ppermute | solution.py:447
  220.2 36.5 %collective-permute-start.14 = (f32[256,4096]{1,0:T(8,128)}, f32[256,4096]{1,0:T(8,128)}, u32[]{:S(2)}, u32[]{:S(2)}) collective-permute-start(f32[256,4096]{1,0:T(8,128)} %get-tuple-element.70), channel_id=1, source_target_pairs={{0,1},{1,0},{2,3},{3,2},{4,5},{5,4},{6,7},{7,6},{8,9},{9,8},{10,11... | collective-permute-start | bytes 12582920 | tf_op jit(solution)/shard_map/ppermute | solution.py:447
  247.8 39.0 %collective-permute-start.17 = (f32[256,4096]{1,0:T(8,128)}, f32[256,4096]{1,0:T(8,128)}, u32[]{:S(2)}, u32[]{:S(2)}) collective-permute-start(f32[256,4096]{1,0:T(8,128)} %get-tuple-element.76), channel_id=1, source_target_pairs={{0,1},{1,0},{2,3},{3,2},{4,5},{5,4},{6,7},{7,6},{8,9},{9,8},{10,11... | collective-permute-start | bytes 12582920 | tf_op jit(solution)/shard_map/ppermute | solution.py:447
  253.7 48.7 %collective-permute-start.19 = (f32[256,2048]{1,0:T(8,128)}, f32[256,2048]{1,0:T(8,128)S(1)}, u32[]{:S(2)}, u32[]{:S(2)}) collective-permute-start(f32[256,2048]{1,0:T(8,128)} %get-tuple-element.81), channel_id=1, source_target_pairs={{0,2},{1,3},{2,0},{3,1},{4,6},{5,7},{6,4},{7,5},{8,10},{9,11},{10,... | collective-permute-start | bytes 6291464 | tf_op jit(solution)/shard_map/ppermute | solution.py:447
  255.2 48.8 %collective-permute-start.20 = (f32[256,2048]{1,0:T(8,128)}, f32[256,2048]{1,0:T(8,128)}, u32[]{:S(2)}, u32[]{:S(2)}) collective-permute-start(f32[256,2048]{1,0:T(8,128)} %get-tuple-element.82), channel_id=1, source_target_pairs={{0,4},{1,5},{2,6},{3,7},{4,0},{5,1},{6,2},{7,3},{8,12},{9,13},{10,... | collective-permute-start | bytes 6291464 | tf_op jit(solution)/shard_map/ppermute | solution.py:447
  285.7 39.2 %collective-permute-start.16 = (f32[128,2048]{1,0:T(8,128)}, f32[128,2048]{1,0:T(8,128)S(1)}, u32[]{:S(2)}, u32[]{:S(2)}) collective-permute-start(f32[128,2048]{1,0:T(8,128)} %get-tuple-element.74), channel_id=1, source_target_pairs={{0,2},{1,3},{2,0},{3,1},{4,6},{5,7},{6,4},{7,5},{8,10},{9,11},{10,... | collective-permute-start | bytes 3145736 | tf_op jit(solution)/shard_map/ppermute | solution.py:447
  286.3 40.2 %collective-permute-start.23 = (f32[128,2048]{1,0:T(8,128)}, f32[128,2048]{1,0:T(8,128)}, u32[]{:S(2)}, u32[]{:S(2)}) collective-permute-start(f32[128,2048]{1,0:T(8,128)} %get-tuple-element.85), channel_id=1, source_target_pairs={{0,4},{1,5},{2,6},{3,7},{4,0},{5,1},{6,2},{7,3},{8,12},{9,13},{10,... | collective-permute-start | bytes 3145736 | tf_op jit(solution)/shard_map/ppermute | solution.py:447
  286.8 121.6 %collective-permute-start.15 = (f32[256,4096]{1,0:T(8,128)}, f32[256,4096]{1,0:T(8,128)}, u32[]{:S(2)}, u32[]{:S(2)}) collective-permute-start(f32[256,4096]{1,0:T(8,128)} %get-tuple-element.73), channel_id=1, source_target_pairs={{0,1},{1,0},{2,3},{3,2},{4,5},{5,4},{6,7},{7,6},{8,9},{9,8},{10,11... | collective-permute-start | bytes 12582920 | tf_op jit(solution)/shard_map/ppermute | solution.py:447
  311.8 96.5 %collective-permute-start.21 = (f32[128,2048]{1,0:T(8,128)}, f32[128,2048]{1,0:T(8,128)}, u32[]{:S(2)}, u32[]{:S(2)}) collective-permute-start(f32[128,2048]{1,0:T(8,128)} %get-tuple-element.83), channel_id=1, source_target_pairs={{0,2},{1,3},{2,0},{3,1},{4,6},{5,7},{6,4},{7,5},{8,10},{9,11},{10,... | collective-permute-start | bytes 3145736 | tf_op jit(solution)/shard_map/ppermute | solution.py:447
  313.1 95.3 %collective-permute-start.24 = (f32[128,2048]{1,0:T(8,128)}, f32[128,2048]{1,0:T(8,128)}, u32[]{:S(2)}, u32[]{:S(2)}) collective-permute-start(f32[128,2048]{1,0:T(8,128)} %get-tuple-element.86), channel_id=1, source_target_pairs={{0,4},{1,5},{2,6},{3,7},{4,0},{5,1},{6,2},{7,3},{8,12},{9,13},{10,... | collective-permute-start | bytes 3145736 | tf_op jit(solution)/shard_map/ppermute | solution.py:447
  324.9 83.5 %collective-permute-start.22 = (f32[2,128,2048]{2,1,0:T(8,128)}, f32[2,128,2048]{2,1,0:T(8,128)S(1)}, u32[]{:S(2)}, u32[]{:S(2)}) collective-permute-start(f32[2,128,2048]{2,1,0:T(8,128)} %get-tuple-element.84), channel_id=1, source_target_pairs={{0,4},{1,5},{2,6},{3,7},{4,0},{5,1},{6,2},{7,3},{8,12},{9,13},{10,... | collective-permute-start | bytes 6291464 | tf_op jit(solution)/shard_map/ppermute | solution.py:447
  326.5 81.9 %collective-permute-start.25 = (f32[2,128,2048]{2,1,0:T(8,128)}, f32[2,128,2048]{2,1,0:T(8,128)}, u32[]{:S(2)}, u32[]{:S(2)}) collective-permute-start(f32[2,128,2048]{2,1,0:T(8,128)} %get-tuple-element.87), channel_id=1, source_target_pairs={{0,2},{1,3},{2,0},{3,1},{4,6},{5,7},{6,4},{7,5},{8,10},{9,11},{10,... | collective-permute-start | bytes 6291464 | tf_op jit(solution)/shard_map/ppermute | solution.py:447
  (10 other events, 262.6 us)

commit v2 on v1

--- a/solution.py
+++ b/solution.py
@@ -11,6 +11,7 @@
 NORM_EPS = 1e-5
 PAD_COLS = 128
 BLK = 512
+VMEM = 67_043_328
 F32 = jnp.float32
 BF16 = jnp.bfloat16
 
@@ -24,7 +25,7 @@
 
 def params(n_axes):
     return pltpu.CompilerParams(
-        dimension_semantics=("arbitrary",) * n_axes, vmem_limit_bytes=60 * 1024 * 1024)
+        dimension_semantics=("arbitrary",) * n_axes, vmem_limit_bytes=VMEM)
 
 
 LOWEST = -3.4028234663852886e38
@@ -32,57 +33,52 @@
 
 def fwd_body(k, n_parts, blk, limit_ref, wt_ref, *refs):
     a_refs = refs[:n_parts]
-    z_ref, stat_ref, hold_ref = refs[-3:]
+    z_ref, stat_ref = refs[-2:]
     step, steps = pl.program_id(0), pl.num_programs(0)
     pairs = [a_refs[i:i + 2] for i in range(0, n_parts, 2)]
     wide = 2 * a_refs[0].shape[0]
 
-    def dots():
-        for i, (lo, hi) in enumerate(pairs):
-            a = jnp.concatenate([lo[...], hi[...]], axis=0)
-            hold_ref[:, i * wide:(i + 1) * wide] = lax.dot_general(
-                wt_ref[...], a, (((1,), (1,)), ((), ())), preferred_element_type=F32)
-
-    def finish():
+    @pl.when(step == 0)
+    def _():
+        stat_ref[...] = jnp.zeros(stat_ref.shape, F32) if k == 0 else refs[n_parts][...]
+        stat_ref[k:k + 1, :] = jnp.full((1, stat_ref.shape[1]), LOWEST, F32)
+        stat_ref[4 + k:5 + k, :] = jnp.zeros((1, stat_ref.shape[1]), F32)
+
+    for i, (lo, hi) in enumerate(pairs):
+        a = jnp.concatenate([lo[...], hi[...]], axis=0)
+        z_ref[:, i * wide:(i + 1) * wide] = lax.dot_general(
+            wt_ref[...], a, (((1,), (1,)), ((), ())), preferred_element_type=F32)
+
+    def finish(masked):
         for i in range(len(pairs)):
             cols = slice(i * wide, (i + 1) * wide)
-            z = hold_ref[:, cols]
-            col = (step - 1) * blk + lax.broadcasted_iota(jnp.int32, z.shape, 0)
-            z = jnp.where(col < limit_ref[0], z, -jnp.inf)
-            z_ref[:, cols] = z
+            z = z_ref[:, cols]
+            if masked:
+                col = step * blk + lax.broadcasted_iota(jnp.int32, z.shape, 0)
+                z = jnp.where(col < limit_ref[0], z, -jnp.inf)
+                z_ref[:, cols] = z
             old = stat_ref[k:k + 1, cols]
             new = jnp.maximum(old, jnp.max(z, axis=0, keepdims=True))
             total = jnp.sum(jnp.exp(z - new), axis=0, keepdims=True)
             stat_ref[k:k + 1, cols] = new
             stat_ref[4 + k:5 + k, cols] = stat_ref[4 + k:5 + k, cols] * jnp.exp(old - new) + total
 
-    @pl.when(step == 0)
-    def _():
-        stat_ref[...] = jnp.zeros(stat_ref.shape, F32) if k == 0 else refs[n_parts][...]
-        stat_ref[k:k + 1, :] = jnp.full((1, stat_ref.shape[1]), LOWEST, F32)
-        stat_ref[4 + k:5 + k, :] = jnp.zeros((1, stat_ref.shape[1]), F32)
-        dots()
-
-    @pl.when((step > 0) & (step < steps - 1))
-    def _():
-        finish()
-        dots()
-
-    pl.when(step == steps - 1)(finish)
+    pl.when(step < steps - 1)(lambda: finish(False))
+    pl.when(step == steps - 1)(lambda: finish(True))
 
 
 def fwd_call(k, parts, wt, limit, stats):
     vocab, dim = wt.shape
     toks = sum(p.shape[0] for p in parts)
     blocks = pl.cdiv(vocab, BLK)
+    assert vocab - (blocks - 1) * BLK > PAD_COLS
     return pl.pallas_call(
         functools.partial(fwd_body, k, len(parts), BLK),
-        grid=(blocks + 1,),
-        in_specs=[pl.BlockSpec(memory_space=pltpu.SMEM), pl.BlockSpec((BLK, dim), lambda j: (jnp.minimum(j, blocks - 1), 0))]
+        grid=(blocks,),
+        in_specs=[pl.BlockSpec(memory_space=pltpu.SMEM), pl.BlockSpec((BLK, dim), lambda j: (j, 0))]
         + [whole(p.shape) for p in parts] + [whole((8, toks))] * len(stats),
-        out_specs=[pl.BlockSpec((BLK, toks), lambda j: (jnp.maximum(j - 1, 0), 0)), whole((8, toks))],
+        out_specs=[pl.BlockSpec((BLK, toks), lambda j: (j, 0)), whole((8, toks))],
         out_shape=[jax.ShapeDtypeStruct((vocab, toks), F32), jax.ShapeDtypeStruct((8, toks), F32)],
-        scratch_shapes=[pltpu.VMEM((BLK, toks), F32)],
         compiler_params=params(1),
         cost_estimate=pl.CostEstimate(
             flops=2 * vocab * dim * toks, bytes_accessed=vocab * dim * 2 + vocab * toks * 4,
@@ -185,9 +181,9 @@
     )(*args)
 
 
-def weight_body(n_parts, dz_ref, *refs):
-    a_refs, out_ref, tick_ref = refs[:n_parts], refs[-2], refs[-1]
-    tick_ref[...] = jnp.zeros_like(tick_ref)
+def weight_body(n_parts, dz_ref, keep_ref, got_ref, *refs):
+    a_refs, out_ref, q_ref = refs[:n_parts], refs[-2], refs[-1]
+    q_ref[...] = keep_ref[...] + got_ref[...]
 
     @pl.loop(0, out_ref.shape[1] // TILE)
     def _(k):
@@ -196,22 +192,24 @@
         out_ref[:, cols] = jnp.dot(dz_ref[...], a, preferred_element_type=F32)
 
 
-def weight_call(dz, parts):
+def weight_call(dz, parts, keep, got):
     vocab, toks = dz.shape
     dim = parts[0].shape[1]
     rows, cols = 1024, dim // 2
+    blocks = pl.cdiv(vocab, rows)
+    share = pl.BlockSpec((keep.shape[0] // (blocks * (dim // cols)), dim), lambda n, j: (n * blocks + j, 0))
     return pl.pallas_call(
         functools.partial(weight_body, len(parts)),
-        grid=(dim // cols, pl.cdiv(vocab, rows)),
-        in_specs=[pl.BlockSpec((rows, toks), lambda n, j: (j, 0))]
+        grid=(dim // cols, blocks),
+        in_specs=[pl.BlockSpec((rows, toks), lambda n, j: (j, 0)), share, share]
         + [pl.BlockSpec((p.shape[0], cols), lambda n, j: (0, n)) for p in parts],
-        out_specs=[pl.BlockSpec((rows, cols), lambda n, j: (j, n)), whole((8, 128))],
-        out_shape=[jax.ShapeDtypeStruct((vocab, dim), F32), jax.ShapeDtypeStruct((8, 128), F32)],
+        out_specs=[pl.BlockSpec((rows, cols), lambda n, j: (j, n)), share],
+        out_shape=[jax.ShapeDtypeStruct((vocab, dim), F32), jax.ShapeDtypeStruct(keep.shape, F32)],
         compiler_params=params(2),
         cost_estimate=pl.CostEstimate(
             flops=2 * vocab * dim * toks, bytes_accessed=vocab * dim * 4 + vocab * toks * 4, transcendentals=0),
         name="dweight",
-    )(dz, *parts)
+    )(dz, keep, got, *parts)
 
 
 def norm_body(hid_ref, gain_ref, lo_ref, hi_ref):
@@ -281,8 +279,13 @@
 
 def sum_body(n, gain_ref, loss_ref, gain_out, loss_out, got_gain, got_loss, send_sem, recv_sem):
     push_all(n, [(gain_ref, got_gain), (loss_ref, got_loss)], send_sem, recv_sem)
-    gain_out[...] = tree([gain_ref[...]] + [got_gain[m] for m in range(1, n)])
-    loss_out[...] = tree([loss_ref[...]] + [got_loss[m] for m in range(1, n)])
+    gain = tree([gain_ref[...]] + [got_gain[m] for m in range(1, n)])
+    per = gain.shape[1] // 128
+    for i in range(gain.shape[0]):
+        for j in range(per):
+            gain_out[i * per + j:i * per + j + 1] = gain[i:i + 1, j * 128:(j + 1) * 128]
+    loss = tree([loss_ref[...]] + [got_loss[m] for m in range(1, n)])
+    loss_out[...] = jnp.sum(loss[0:1], axis=1, keepdims=True)
 
 
 LAYOUT = (
@@ -396,14 +399,12 @@
     )(keep, keep, got, got, sa, ta, x, x, y, y)
 
 
-def last_body(hid_ref, gain_ref, keep_ref, got_ref, x2a_ref, x2b_ref, s4_ref, y4a_ref, y4b_ref, t2_ref, tick_ref,
-              dh_ref, dgain_ref):
-    del tick_ref
+def last_body(hid_ref, gain_ref, q_ref, x2a_ref, x2b_ref, s4_ref, y4a_ref, y4b_ref, t2_ref, dh_ref, dgain_ref):
     step = pl.program_id(0)
     dhalf = s4_ref.shape[1]
 
     def run(x2_ref, y4_ref):
-        q = keep_ref[...] + got_ref[...]
+        q = q_ref[...]
         g = jnp.concatenate(
             [q[:, :dhalf] + x2_ref[...] + s4_ref[...], q[:, dhalf:] + y4_ref[...] + t2_ref[...]], axis=1)
         x = hid_ref[...].astype(F32)
@@ -421,9 +422,9 @@
     pl.when(step >= pl.num_programs(0) // 2)(lambda: run(x2b_ref, y4b_ref))
 
 
-def last_call(hidden, gain, keep, got, x2a, x2b, s4, y4a, y4b, t2, tick):
+def last_call(hidden, gain, q, x2a, x2b, s4, y4a, y4b, t2):
     rows, dim = hidden.shape
-    steps = 8
+    steps = 4
     blk, mid, dhalf = rows // steps, steps // 2, dim // 2
     row = lambda width: pl.BlockSpec((blk, width), lambda i: (i, 0))
     low = pl.BlockSpec((blk, dhalf), lambda i: (jnp.minimum(i, mid - 1), 0))
@@ -431,13 +432,13 @@
     return pl.pallas_call(
         last_body,
         grid=(steps,),
-        in_specs=[row(dim), whole((1, dim)), row(dim), row(dim), low, high, row(dhalf), low, high, row(dhalf), ANY],
+        in_specs=[row(dim), whole((1, dim)), row(dim), low, high, row(dhalf), low, high, row(dhalf)],
         out_specs=[row(dim), whole((8, dim // 8))],
         out_shape=[jax.ShapeDtypeStruct((rows, dim), BF16), jax.ShapeDtypeStruct((8, dim // 8), F32)],
         compiler_params=params(1),
         cost_estimate=pl.CostEstimate(flops=20 * rows * dim, bytes_accessed=rows * dim * 20, transcendentals=rows),
         name="last",
-    )(hidden, gain[None], keep, got, x2a, x2b, s4, y4a, y4b, t2, tick)
+    )(hidden, gain[None], q, x2a, x2b, s4, y4a, y4b, t2)
 
 
 def solution(mesh):
@@ -497,11 +498,11 @@
         x2b, y4b = swap(x2b, 2), swap(y4b, 4)
         s4, t2 = swap(s4, 4).reshape(rows, dhalf), swap(t2, 2).reshape(rows, dhalf)
 
-        dwt, tick = weight_call(dz, [p for g in groups for p in g])
-        d_input, d_gain = last_call(hidden, norm_gain, keep0, got0, x2a, x2b, s4, y4a, y4b, t2, tick)
+        dwt, q0 = weight_call(dz, [p for g in groups for p in g], keep0, got0)
+        d_input, d_gain = last_call(hidden, norm_gain, q0, x2a, x2b, s4, y4a, y4b, t2)
         d_gain, loss = small_call(
-            functools.partial(sum_body, n), n, [d_gain, loss], [spec(d_gain.shape, F32), spec(loss.shape, F32)], 1)
-        return jnp.sum(loss[0]).reshape(1), d_input, dwt.T, d_gain.reshape(dim)
+            functools.partial(sum_body, n), n, [d_gain, loss], [spec((dim // 128, 128), F32), spec((1, 1), F32)], 1)
+        return loss.reshape(1), d_input, dwt.T, d_gain.reshape(dim)
 
     return jax.shard_map(
         compute,

time: 439 us -> 469 us (1.068)
  waiting for transfers between devices: 72.1 us -> 102 us
    ppermute x26, waiting for transfers between devices: 72.1 us -> 102 us  [swap(): return lax.ppermute(v, 'vp', [(i, i ^ mask) for i in range(n)])]
  transfers between devices with their start and end apart: 26 -> 26, of which waited for: 7 -> 6; matrix products, arithmetic and copies ran while one was open for 0% -> 0% of each run, Pallas kernels for 58% -> 50%
where the time goes in v2:
time: 469 us; the launch traced here: 460 us
  Pallas kernels  336 us (72%)
  waiting for transfers between devices  102 us (22%)
  starting transfers between devices  19.1 us (4%)
    pallas_call x4, Pallas kernels, back_call(): pl.pallas_call(functools.partial(back_body, k, mixing, BLK, vocab), grid=...  111 us
    pallas_call x4, Pallas kernels, fwd_call(): pl.pallas_call(functools.partial(fwd_body, k, len(parts), BLK), grid=(blo...  102 us
    ppermute x26, waiting for transfers between devices, swap(): return lax.ppermute(v, 'vp', [(i, i ^ mask) for i in range(n)])  102 us
    pallas_call x1, Pallas kernels, weight_call(): pl.pallas_call(functools.partial(weight_body, len(parts)), grid=(dim // c...  81.5 us
    ppermute x26, starting transfers between devices, swap(): return lax.ppermute(v, 'vp', [(i, i ^ mask) for i in range(n)])  19.1 us
    pallas_call x2, Pallas kernels, small_call(): pl.pallas_call(body, in_specs=[vm] * len(args), out_specs=[vm] * len(outs...  14.9 us
  transfers between devices with their start and end apart: 26, of which 6 were waited for; matrix products, arithmetic and copies ran while one was open for 0% of the time, Pallas kernels for 50%

profile of v2, /device:TPU:0, one launch (start us, length us, event | category | flops | bytes accessed | tf_op | source)
XLA Modules:
  0.0 460.4 jit_solution(1436362169396524741)
XLA Ops:
  0.6 3.8 norm.1
  5.2 2.5 collective-permute-start
  7.7 1.5 collective-permute-start.9
  10.7 21.3 %collective-permute-done.refs_0_.refs_4_ = bf16[128,4096]{1,0:T(8,128)(2,1)} collective-permute-done((bf16[128,4096]{1,0:T(8,128)(2,1)}, bf16[128,4096]{1,0:T(8,128)(2,1)}, u32[]{:S(2)}, u32[]{:S(2)}) %collective-permute-start) | collective-permute-done | bytes 1048608 | tf_op jit(solution)/shard_map/ppermute | solution.py:448
  32.0 2.0 collective-permute-done.9.refs_1_.refs_5_
  35.5 20.9 %collective-permute-done.2.refs_1_.refs_9_ = bf16[128,4096]{1,0:T(8,128)(2,1)} collective-permute-done((bf16[128,4096]{1,0:T(8,128)(2,1)}, bf16[128,4096]{1,0:T(8,128)(2,1)}, u32[]{:S(2)}, u32[]{:S(2)}) %collective-permute-start.2) | collective-permute-done | bytes 1048608 | tf_op jit(solution)/shard_map/ppermute | solution.py:448
  56.5 25.6 %fwd.4 = (f32[4016,512]{1,0:T(8,128)}, f32[8,512]{1,0:T(8,128)}) custom-call(s32[1]{0:T(128)} %bitcast.1.limit_ref, bf16[4016,4096]{1,0:T(8,128)(2,1)} %bitcast.10, bf16[128,4096]{1,0:T(8,128)(2,1)} %get-tuple-element.50.refs_0_, bf16[128,4096]{1,0:T(8,128)(2,1)} %get-tuple-element.51.refs_1_, bf16[128,4096]{1,0:T(8,128)(2,1)} %collective-permute-done.12.refs_2_, ...), custom_call_target="tpu_custom_call" | custom-call | flops 16844324864 | bytes 41123840 | tf_op jit(solution)/shard_map/fwd/pallas_call | solution.py:75
  83.2 25.6 %fwd.5 = (f32[4016,512]{1,0:T(8,128)}, f32[8,512]{1,0:T(8,128)}) custom-call(s32[1]{0:T(128)} %bitcast.1.limit_ref, bf16[4016,4096]{1,0:T(8,128)(2,1)} %bitcast.11, bf16[128,4096]{1,0:T(8,128)(2,1)} %collective-permute-done.refs_0_.refs_4_, bf16[128,4096]{1,0:T(8,128)(2,1)} %collective-permute-done.9.refs_1_.refs_5_, ...), custom_call_target="tpu_custom_call" | custom-call | flops 16844324864 | bytes 41123840 | tf_op jit(solution)/shard_map/fwd/pallas_call | solution.py:75
  108.8 25.7 %fwd.6 = (f32[4016,512]{1,0:T(8,128)}, f32[8,512]{1,0:T(8,128)}) custom-call(s32[1]{0:T(128)} %bitcast.1.limit_ref, bf16[4016,4096]{1,0:T(8,128)(2,1)} %bitcast.12, bf16[128,4096]{1,0:T(8,128)(2,1)} %collective-permute-done.6.refs_0_.refs_8_, bf16[128,4096]{1,0:T(8,128)(2,1)} %collective-permute-done.2.refs_1_.refs_9_, ...), custom_call_target="tpu_custom_call" | custom-call | flops 16844324864 | bytes 41123840 | tf_op jit(solution)/shard_map/fwd/pallas_call | solution.py:75
  134.5 25.6 %fwd.7 = (f32[4016,512]{1,0:T(8,128)}, f32[8,512]{1,0:T(8,128)}) custom-call(s32[1]{0:T(128)} %bitcast.1.limit_ref, bf16[4016,4096]{1,0:T(8,128)(2,1)} %bitcast.13, bf16[128,4096]{1,0:T(8,128)(2,1)} %collective-permute-done.1.refs_0_.refs_12_, bf16[128,4096]{1,0:T(8,128)(2,1)} %collective-permute-done.3.refs_1_.refs_13_, ...), custom_call_target="tpu_custom_call" | custom-call | flops 16844324864 | bytes 41123840 | tf_op jit(solution)/shard_map/fwd/pallas_call | solution.py:75
  160.1 7.8 %shard_map.84 = (s32[8,512]{1,0:T(8,128)}, f32[8,512]{1,0:T(8,128)}, f32[8,512]{1,0:T(8,128)}, f32[8,128]{1,0:T(8,128)}) custom-call(f32[8,512]{1,0:T(8,128)} %get-tuple-element.55.stat_ref, s32[2,128]{1,0:T(2,128)} %bitcast.21, f32[2,128]{1,0:T(2,128)} %bitcast.22), custom_call_target="tpu_custom_call" | custom-call | flops 4000 | bytes 4000000 | tf_op jit(solution)/shard_map/pallas_call | solution.py:336
  167.9 27.4 %back.4 = (bf16[4016,2048]{1,0:T(8,128)(2,1)}, f32[256,4096]{1,0:T(8,128)}, f32[256,4096]{1,0:T(8,128)}, f32[8,128]{1,0:T(8,128)}) custom-call(s32[8,512]{1,0:T(8,128)} %get-tuple-element.56.label_ref, f32[8,512]{1,0:T(8,128)} %get-tuple-element.57.lse_ref, f32[8,512]{1,0:T(8,128)} %get-tuple-element.58.scale_ref, f32[8,128]{1,0:T(8,128)} %get-tuple-element.59.loss_ref, ...), custom_call_target="tpu_custom_call" | custom-call | flops 16844324864 | bytes 45236224 | tf_op jit(solution)/shard_map/back/pallas_call | solution.py:168
  195.3 26.9 %back.5 = (bf16[4016,2048]{1,0:T(8,128)(2,1)}, f32[256,4096]{1,0:T(8,128)}, f32[256,4096]{1,0:T(8,128)}, f32[8,128]{1,0:T(8,128)}) custom-call(s32[8,512]{1,0:T(8,128)} %get-tuple-element.56.label_ref, f32[8,512]{1,0:T(8,128)} %get-tuple-element.57.lse_ref, f32[8,512]{1,0:T(8,128)} %get-tuple-element.58.scale_ref, ...), custom_call_target="tpu_custom_call", output_to_operand_aliasing={{0}: (6, {})} | custom-call | flops 16844324864 | bytes 45236224 | tf_op jit(solution)/shard_map/back/pallas_call | solution.py:168
  222.8 27.1 %back.6 = (bf16[4016,2048]{1,0:T(8,128)(2,1)}, f32[256,4096]{1,0:T(8,128)}, f32[256,4096]{1,0:T(8,128)}, f32[8,128]{1,0:T(8,128)}) custom-call(s32[8,512]{1,0:T(8,128)} %get-tuple-element.56.label_ref, f32[8,512]{1,0:T(8,128)} %get-tuple-element.57.lse_ref, f32[8,512]{1,0:T(8,128)} %get-tuple-element.58.scale_ref, ...), custom_call_target="tpu_custom_call", output_to_operand_aliasing={{0}: (6, {})} | custom-call | flops 16844324864 | bytes 45236224 | tf_op jit(solution)/shard_map/back/pallas_call | solution.py:168
  250.1 29.1 %back.7 = (bf16[4016,2048]{1,0:T(8,128)(2,1)}, f32[256,4096]{1,0:T(8,128)}, f32[256,4096]{1,0:T(8,128)}, f32[8,128]{1,0:T(8,128)}, f32[128,2048]{1,0:T(8,128)}, ...) custom-call(s32[8,512]{1,0:T(8,128)} %get-tuple-element.56.label_ref, ...), custom_call_target="tpu_custom_call", output_to_operand_aliasing={{0}: (8, {})} | custom-call | flops 16844324864 | bytes 45236224 | tf_op jit(solution)/shard_map/back/pallas_call | solution.py:168
  279.6 5.7 %mix.1 = (f32[256,2048]{1,0:T(8,128)}, f32[256,2048]{1,0:T(8,128)}) custom-call(f32[256,4096]{1,0:T(8,128)} %get-tuple-element.81.keep_ref, f32[256,4096]{1,0:T(8,128)} %collective-permute-done.18.got_ref), custom_call_target="tpu_custom_call" | custom-call | flops 1048576 | bytes 12582912 | tf_op jit(solution)/shard_map/mix/pallas_call | solution.py:358
  289.4 44.8 %collective-permute-done.19.xa_ref.xb_ref = f32[256,2048]{1,0:T(8,128)} collective-permute-done((f32[256,2048]{1,0:T(8,128)}, f32[256,2048]{1,0:T(8,128)}, u32[]{:S(2)}, u32[]{:S(2)}) %collective-permute-start.19) | collective-permute-done | bytes 2097184 | tf_op jit(solution)/shard_map/ppermute | solution.py:448
  335.7 7.8 %second.1 = (f32[128,2048]{1,0:T(8,128)}, f32[128,2048]{1,0:T(8,128)}, f32[2,128,2048]{2,1,0:T(8,128)}, f32[2,128,2048]{2,1,0:T(8,128)}) custom-call(f32[256,4096]{1,0:T(8,128)} %get-tuple-element.77.keep2_ref.keep4_ref, f32[256,4096]{1,0:T(8,128)} %get-tuple-element.77.keep2_ref.keep4_ref, f32[256,4096]{1,0:T(8,128)} %collective-permute-done.17.got2_ref.got4_ref, ...), custom_call_target="tpu_custom_call" | custom-call | flops 2097152 | bytes 20971520 | tf_op jit(solution)/shard_map/second/pallas_call | solution.py:389
  344.0 1.5 collective-permute-start.24
  345.6 11.1 %collective-permute-done.16.x2a_ref = f32[128,2048]{1,0:T(8,128)} collective-permute-done((f32[128,2048]{1,0:T(8,128)}, f32[128,2048]{1,0:T(8,128)}, u32[]{:S(2)}, u32[]{:S(2)}) %collective-permute-start.16) | collective-permute-done | bytes 1048608 | tf_op jit(solution)/shard_map/ppermute | solution.py:448
  356.7 1.5 collective-permute-start.22
  359.6 81.5 %dweight.1 = (f32[4016,4096]{1,0:T(8,128)}, f32[256,4096]{1,0:T(8,128)}) custom-call(bf16[4016,2048]{1,0:T(8,128)(2,1)} %get-tuple-element.72.dz_ref, f32[256,4096]{1,0:T(8,128)} %get-tuple-element.73.keep_ref, f32[256,4096]{1,0:T(8,128)} %collective-permute-done.15.got_ref, bf16[128,4096]{1,0:T(8,128)(2,1)} %get-tuple-element.50.refs_0_, ...), custom_call_target="tpu_custom_call" | custom-call | flops 67377299456 | bytes 98697216 | tf_op jit(solution)/shard_map/dweight/pallas_call | solution.py:201
  441.2 8.9 %last.1 = (bf16[256,4096]{1,0:T(8,128)(2,1)}, f32[8,512]{1,0:T(8,128)}) custom-call(bf16[256,4096]{1,0:T(8,128)(2,1)} %hid_ref.1, f32[1,4096]{1,0:T(1,128)} %bitcast.19, f32[256,4096]{1,0:T(8,128)} %get-tuple-element.75.q_ref, f32[128,2048]{1,0:T(8,128)} %collective-permute-done.16.x2a_ref, f32[128,2048]{1,0:T(8,128)} %collective-permute-done.21.x2b_ref, ...), custom_call_target="tpu_custom_call" | custom-call | flops 20971520 | bytes 20971520 | tf_op jit(solution)/shard_map/last/pallas_call | solution.py:432
  450.1 7.1 %shard_map.85 = (f32[32,128]{1,0:T(8,128)}, f32[1,1]{1,0:T(1,128)}) custom-call(f32[8,512]{1,0:T(8,128)} %get-tuple-element.90.gain_ref, f32[8,128]{1,0:T(8,128)} %get-tuple-element.91.loss_ref), custom_call_target="tpu_custom_call" | custom-call | flops 4000 | bytes 4000000 | tf_op jit(solution)/shard_map/pallas_call | solution.py:336
  (44 shorter events, 14.9 us)
Async XLA Ops:
  5.2 26.8 %collective-permute-start = (bf16[128,4096]{1,0:T(8,128)(2,1)}, bf16[128,4096]{1,0:T(8,128)(2,1)}, u32[]{:S(2)}, u32[]{:S(2)}) collective-permute-start(bf16[128,4096]{1,0:T(8,128)(2,1)} %get-tuple-element.50.refs_0_), channel_id=1, source_target_pairs={{0,2},{1,3},{2,0},{3,1},{4,6},{5,7},{6,4},{7,5},{8,10},{9,11},{10,... | collective-permute-start | bytes 3145736 | tf_op jit(solution)/shard_map/ppermute | solution.py:448
  7.7 26.3 %collective-permute-start.9 = (bf16[128,4096]{1,0:T(8,128)(2,1)}, bf16[128,4096]{1,0:T(8,128)(2,1)}, u32[]{:S(2)}, u32[]{:S(2)}) collective-permute-start(bf16[128,4096]{1,0:T(8,128)(2,1)} %get-tuple-element.50.refs_0_), channel_id=1, source_target_pairs={{0,4},{1,5},{2,6},{3,7},{4,0},{5,1},{6,2},{7,3},{8,12},{9,13},{10,... | collective-permute-start | bytes 3145736 | tf_op jit(solution)/shard_map/ppermute | solution.py:448
  9.2 26.4 %collective-permute-start.13 = (bf16[128,4096]{1,0:T(8,128)(2,1)}, bf16[128,4096]{1,0:T(8,128)(2,1)}, u32[]{:S(2)}, u32[]{:S(2)}) collective-permute-start(bf16[128,4096]{1,0:T(8,128)(2,1)} %get-tuple-element.51.refs_1_), channel_id=1, source_target_pairs={{0,1},{1,0},{2,3},{3,2},{4,5},{5,4},{6,7},{7,6},{8,9},{9,8},{10,11... | collective-permute-start | bytes 3145736 | tf_op jit(solution)/shard_map/ppermute | solution.py:448
  9.2 47.3 %collective-permute-start.2 = (bf16[128,4096]{1,0:T(8,128)(2,1)}, bf16[128,4096]{1,0:T(8,128)(2,1)}, u32[]{:S(2)}, u32[]{:S(2)}) collective-permute-start(bf16[128,4096]{1,0:T(8,128)(2,1)} %get-tuple-element.51.refs_1_), channel_id=1, source_target_pairs={{0,4},{1,5},{2,6},{3,7},{4,0},{5,1},{6,2},{7,3},{8,12},{9,13},{10,... | collective-permute-start | bytes 3145736 | tf_op jit(solution)/shard_map/ppermute | solution.py:448
  9.7 72.4 %collective-permute-start.6 = (bf16[128,4096]{1,0:T(8,128)(2,1)}, bf16[128,4096]{1,0:T(8,128)(2,1)}, u32[]{:S(2)}, u32[]{:S(2)}) collective-permute-start(bf16[128,4096]{1,0:T(8,128)(2,1)} %get-tuple-element.51.refs_1_), channel_id=1, source_target_pairs={{0,2},{1,3},{2,0},{3,1},{4,6},{5,7},{6,4},{7,5},{8,10},{9,11},{10,... | collective-permute-start | bytes 3145736 | tf_op jit(solution)/shard_map/ppermute | solution.py:448
  32.0 51.2 %collective-permute-start.10 = (bf16[128,4096]{1,0:T(8,128)(2,1)}, bf16[128,4096]{1,0:T(8,128)(2,1)}, u32[]{:S(2)}, u32[]{:S(2)}) collective-permute-start(bf16[128,4096]{1,0:T(8,128)(2,1)} %collective-permute-done.refs_0_.refs_4_), channel_id=1, source_target_pairs={{0,1},{1,0},{2,3},{3,2},{4,5},{5,4},{6,7},{7,6},{8,9},{9,8},{10,11... | collective-permute-start | bytes 3145736 | tf_op jit(solution)/shard_map/ppermute | solution.py:448
  34.0 48.6 %collective-permute-start.1 = (bf16[128,4096]{1,0:T(8,128)(2,1)}, bf16[128,4096]{1,0:T(8,128)(2,1)}, u32[]{:S(2)}, u32[]{:S(2)}) collective-permute-start(bf16[128,4096]{1,0:T(8,128)(2,1)} %collective-permute-done.refs_0_.refs_4_), channel_id=1, source_target_pairs={{0,4},{1,5},{2,6},{3,7},{4,0},{5,1},{6,2},{7,3},{8,12},{9,13},{10,... | collective-permute-start | bytes 3145736 | tf_op jit(solution)/shard_map/ppermute | solution.py:448
  35.5 46.6 %collective-permute-start.11 = (bf16[128,4096]{1,0:T(8,128)(2,1)}, bf16[128,4096]{1,0:T(8,128)(2,1)}, u32[]{:S(2)}, u32[]{:S(2)}) collective-permute-start(bf16[128,4096]{1,0:T(8,128)(2,1)} %collective-permute-done.9.refs_1_.refs_5_), channel_id=1, source_target_pairs={{0,1},{1,0},{2,3},{3,2},{4,5},{5,4},{6,7},{7,6},{8,9},{9,8},{10,11... | collective-permute-start | bytes 3145736 | tf_op jit(solution)/shard_map/ppermute | solution.py:448
  82.1 26.7 %collective-permute-start.8 = (bf16[128,4096]{1,0:T(8,128)(2,1)}, bf16[128,4096]{1,0:T(8,128)(2,1)}, u32[]{:S(2)}, u32[]{:S(2)}) collective-permute-start(bf16[128,4096]{1,0:T(8,128)(2,1)} %collective-permute-done.2.refs_1_.refs_9_), channel_id=1, source_target_pairs={{0,1},{1,0},{2,3},{3,2},{4,5},{5,4},{6,7},{7,6},{8,9},{9,8},{10,11... | collective-permute-start | bytes 3145736 | tf_op jit(solution)/shard_map/ppermute | solution.py:448
  82.2 26.6 %collective-permute-start.7 = (bf16[128,4096]{1,0:T(8,128)(2,1)}, bf16[128,4096]{1,0:T(8,128)(2,1)}, u32[]{:S(2)}, u32[]{:S(2)}) collective-permute-start(bf16[128,4096]{1,0:T(8,128)(2,1)} %collective-permute-done.6.refs_0_.refs_8_), channel_id=1, source_target_pairs={{0,1},{1,0},{2,3},{3,2},{4,5},{5,4},{6,7},{7,6},{8,9},{9,8},{10,11... | collective-permute-start | bytes 3145736 | tf_op jit(solution)/shard_map/ppermute | solution.py:448
  82.7 51.8 %collective-permute-start.4 = (bf16[128,4096]{1,0:T(8,128)(2,1)}, bf16[128,4096]{1,0:T(8,128)(2,1)}, u32[]{:S(2)}, u32[]{:S(2)}) collective-permute-start(bf16[128,4096]{1,0:T(8,128)(2,1)} %collective-permute-done.1.refs_0_.refs_12_), channel_id=1, source_target_pairs={{0,1},{1,0},{2,3},{3,2},{4,5},{5,4},{6,7},{7,6},{8,9},{9,8},{10,11... | collective-permute-start | bytes 3145736 | tf_op jit(solution)/shard_map/ppermute | solution.py:448
  82.7 51.8 %collective-permute-start.5 = (bf16[128,4096]{1,0:T(8,128)(2,1)}, bf16[128,4096]{1,0:T(8,128)(2,1)}, u32[]{:S(2)}, u32[]{:S(2)}) collective-permute-start(bf16[128,4096]{1,0:T(8,128)(2,1)} %collective-permute-done.3.refs_1_.refs_13_), channel_id=1, source_target_pairs={{0,1},{1,0},{2,3},{3,2},{4,5},{5,4},{6,7},{7,6},{8,9},{9,8},{10,11... | collective-permute-start | bytes 3145736 | tf_op jit(solution)/shard_map/ppermute | solution.py:448
  222.3 27.8 %collective-permute-start.14 = (f32[256,4096]{1,0:T(8,128)}, f32[256,4096]{1,0:T(8,128)}, u32[]{:S(2)}, u32[]{:S(2)}) collective-permute-start(f32[256,4096]{1,0:T(8,128)} %get-tuple-element.70), channel_id=1, source_target_pairs={{0,1},{1,0},{2,3},{3,2},{4,5},{5,4},{6,7},{7,6},{8,9},{9,8},{10,11... | collective-permute-start | bytes 12582920 | tf_op jit(solution)/shard_map/ppermute | solution.py:448
  222.4 57.3 %collective-permute-start.18 = (f32[256,4096]{1,0:T(8,128)}, f32[256,4096]{1,0:T(8,128)}, u32[]{:S(2)}, u32[]{:S(2)}) collective-permute-start(f32[256,4096]{1,0:T(8,128)} %get-tuple-element.82), channel_id=1, source_target_pairs={{0,1},{1,0},{2,3},{3,2},{4,5},{5,4},{6,7},{7,6},{8,9},{9,8},{10,11... | collective-permute-start | bytes 12582920 | tf_op jit(solution)/shard_map/ppermute | solution.py:448
  249.9 39.0 %collective-permute-start.17 = (f32[256,4096]{1,0:T(8,128)}, f32[256,4096]{1,0:T(8,128)}, u32[]{:S(2)}, u32[]{:S(2)}) collective-permute-start(f32[256,4096]{1,0:T(8,128)} %get-tuple-element.78), channel_id=1, source_target_pairs={{0,1},{1,0},{2,3},{3,2},{4,5},{5,4},{6,7},{7,6},{8,9},{9,8},{10,11... | collective-permute-start | bytes 12582920 | tf_op jit(solution)/shard_map/ppermute | solution.py:448
  279.2 79.0 %collective-permute-start.15 = (f32[256,4096]{1,0:T(8,128)}, f32[256,4096]{1,0:T(8,128)}, u32[]{:S(2)}, u32[]{:S(2)}) collective-permute-start(f32[256,4096]{1,0:T(8,128)} %get-tuple-element.74), channel_id=1, source_target_pairs={{0,1},{1,0},{2,3},{3,2},{4,5},{5,4},{6,7},{7,6},{8,9},{9,8},{10,11... | collective-permute-start | bytes 12582920 | tf_op jit(solution)/shard_map/ppermute | solution.py:448
  285.4 48.8 %collective-permute-start.19 = (f32[256,2048]{1,0:T(8,128)}, f32[256,2048]{1,0:T(8,128)}, u32[]{:S(2)}, u32[]{:S(2)}) collective-permute-start(f32[256,2048]{1,0:T(8,128)} %get-tuple-element.83), channel_id=1, source_target_pairs={{0,2},{1,3},{2,0},{3,1},{4,6},{5,7},{6,4},{7,5},{8,10},{9,11},{10,... | collective-permute-start | bytes 6291464 | tf_op jit(solution)/shard_map/ppermute | solution.py:448
  286.9 48.8 %collective-permute-start.20 = (f32[256,2048]{1,0:T(8,128)}, f32[256,2048]{1,0:T(8,128)}, u32[]{:S(2)}, u32[]{:S(2)}) collective-permute-start(f32[256,2048]{1,0:T(8,128)} %get-tuple-element.84), channel_id=1, source_target_pairs={{0,4},{1,5},{2,6},{3,7},{4,0},{5,1},{6,2},{7,3},{8,12},{9,13},{10,... | collective-permute-start | bytes 6291464 | tf_op jit(solution)/shard_map/ppermute | solution.py:448
  288.3 68.3 %collective-permute-start.16 = (f32[128,2048]{1,0:T(8,128)}, f32[128,2048]{1,0:T(8,128)}, u32[]{:S(2)}, u32[]{:S(2)}) collective-permute-start(f32[128,2048]{1,0:T(8,128)} %get-tuple-element.76), channel_id=1, source_target_pairs={{0,2},{1,3},{2,0},{3,1},{4,6},{5,7},{6,4},{7,5},{8,10},{9,11},{10,... | collective-permute-start | bytes 3145736 | tf_op jit(solution)/shard_map/ppermute | solution.py:448
  289.0 152.2 %collective-permute-start.23 = (f32[128,2048]{1,0:T(8,128)}, f32[128,2048]{1,0:T(8,128)}, u32[]{:S(2)}, u32[]{:S(2)}) collective-permute-start(f32[128,2048]{1,0:T(8,128)} %get-tuple-element.87), channel_id=1, source_target_pairs={{0,4},{1,5},{2,6},{3,7},{4,0},{5,1},{6,2},{7,3},{8,12},{9,13},{10,... | collective-permute-start | bytes 3145736 | tf_op jit(solution)/shard_map/ppermute | solution.py:448
  343.5 97.7 %collective-permute-start.21 = (f32[128,2048]{1,0:T(8,128)}, f32[128,2048]{1,0:T(8,128)}, u32[]{:S(2)}, u32[]{:S(2)}) collective-permute-start(f32[128,2048]{1,0:T(8,128)} %get-tuple-element.85), channel_id=1, source_target_pairs={{0,2},{1,3},{2,0},{3,1},{4,6},{5,7},{6,4},{7,5},{8,10},{9,11},{10,... | collective-permute-start | bytes 3145736 | tf_op jit(solution)/shard_map/ppermute | solution.py:448
  344.0 97.1 %collective-permute-start.24 = (f32[128,2048]{1,0:T(8,128)}, f32[128,2048]{1,0:T(8,128)}, u32[]{:S(2)}, u32[]{:S(2)}) collective-permute-start(f32[128,2048]{1,0:T(8,128)} %get-tuple-element.88), channel_id=1, source_target_pairs={{0,4},{1,5},{2,6},{3,7},{4,0},{5,1},{6,2},{7,3},{8,12},{9,13},{10,... | collective-permute-start | bytes 3145736 | tf_op jit(solution)/shard_map/ppermute | solution.py:448
  356.7 84.5 %collective-permute-start.22 = (f32[2,128,2048]{2,1,0:T(8,128)}, f32[2,128,2048]{2,1,0:T(8,128)}, u32[]{:S(2)}, u32[]{:S(2)}) collective-permute-start(f32[2,128,2048]{2,1,0:T(8,128)} %get-tuple-element.86), channel_id=1, source_target_pairs={{0,4},{1,5},{2,6},{3,7},{4,0},{5,1},{6,2},{7,3},{8,12},{9,13},{10,... | collective-permute-start | bytes 6291464 | tf_op jit(solution)/shard_map/ppermute | solution.py:448
  358.2 83.0 %collective-permute-start.25 = (f32[2,128,2048]{2,1,0:T(8,128)}, f32[2,128,2048]{2,1,0:T(8,128)}, u32[]{:S(2)}, u32[]{:S(2)}) collective-permute-start(f32[2,128,2048]{2,1,0:T(8,128)} %get-tuple-element.89), channel_id=1, source_target_pairs={{0,2},{1,3},{2,0},{3,1},{4,6},{5,7},{6,4},{7,5},{8,10},{9,11},{10,... | collective-permute-start | bytes 6291464 | tf_op jit(solution)/shard_map/ppermute | solution.py:448
  (2 other events, 31.5 us)

commit v3 on v2

--- a/solution.py
+++ b/solution.py
@@ -11,6 +11,7 @@
 NORM_EPS = 1e-5
 PAD_COLS = 128
 BLK = 512
+BACK_BLK = 1024
 VMEM = 67_043_328
 F32 = jnp.float32
 BF16 = jnp.bfloat16
@@ -33,37 +34,43 @@
 
 def fwd_body(k, n_parts, blk, limit_ref, wt_ref, *refs):
     a_refs = refs[:n_parts]
-    z_ref, stat_ref = refs[-2:]
+    z_ref, stat_ref, hold_ref = refs[-3:]
     step, steps = pl.program_id(0), pl.num_programs(0)
     pairs = [a_refs[i:i + 2] for i in range(0, n_parts, 2)]
     wide = 2 * a_refs[0].shape[0]
 
-    @pl.when(step == 0)
-    def _():
-        stat_ref[...] = jnp.zeros(stat_ref.shape, F32) if k == 0 else refs[n_parts][...]
-        stat_ref[k:k + 1, :] = jnp.full((1, stat_ref.shape[1]), LOWEST, F32)
-        stat_ref[4 + k:5 + k, :] = jnp.zeros((1, stat_ref.shape[1]), F32)
-
-    for i, (lo, hi) in enumerate(pairs):
-        a = jnp.concatenate([lo[...], hi[...]], axis=0)
-        z_ref[:, i * wide:(i + 1) * wide] = lax.dot_general(
-            wt_ref[...], a, (((1,), (1,)), ((), ())), preferred_element_type=F32)
+    def dots():
+        for i, (lo, hi) in enumerate(pairs):
+            a = jnp.concatenate([lo[...], hi[...]], axis=0)
+            hold_ref[:, i * wide:(i + 1) * wide] = lax.dot_general(
+                wt_ref[...], a, (((1,), (1,)), ((), ())), preferred_element_type=F32)
 
     def finish(masked):
         for i in range(len(pairs)):
             cols = slice(i * wide, (i + 1) * wide)
-            z = z_ref[:, cols]
+            z = hold_ref[:, cols]
             if masked:
-                col = step * blk + lax.broadcasted_iota(jnp.int32, z.shape, 0)
+                col = (step - 1) * blk + lax.broadcasted_iota(jnp.int32, z.shape, 0)
                 z = jnp.where(col < limit_ref[0], z, -jnp.inf)
-                z_ref[:, cols] = z
+            z_ref[:, cols] = z
             old = stat_ref[k:k + 1, cols]
             new = jnp.maximum(old, jnp.max(z, axis=0, keepdims=True))
             total = jnp.sum(jnp.exp(z - new), axis=0, keepdims=True)
             stat_ref[k:k + 1, cols] = new
             stat_ref[4 + k:5 + k, cols] = stat_ref[4 + k:5 + k, cols] * jnp.exp(old - new) + total
 
-    pl.when(step < steps - 1)(lambda: finish(False))
+    @pl.when(step == 0)
+    def _():
+        stat_ref[...] = jnp.zeros(stat_ref.shape, F32) if k == 0 else refs[n_parts][...]
+        stat_ref[k:k + 1, :] = jnp.full((1, stat_ref.shape[1]), LOWEST, F32)
+        stat_ref[4 + k:5 + k, :] = jnp.zeros((1, stat_ref.shape[1]), F32)
+        dots()
+
+    @pl.when((step > 0) & (step < steps - 1))
+    def _():
+        finish(False)
+        dots()
+
     pl.when(step == steps - 1)(lambda: finish(True))
 
 
@@ -74,11 +81,12 @@
     assert vocab - (blocks - 1) * BLK > PAD_COLS
     return pl.pallas_call(
         functools.partial(fwd_body, k, len(parts), BLK),
-        grid=(blocks,),
-        in_specs=[pl.BlockSpec(memory_space=pltpu.SMEM), pl.BlockSpec((BLK, dim), lambda j: (j, 0))]
+        grid=(blocks + 1,),
+        in_specs=[pl.BlockSpec(memory_space=pltpu.SMEM), pl.BlockSpec((BLK, dim), lambda j: (jnp.minimum(j, blocks - 1), 0))]
         + [whole(p.shape) for p in parts] + [whole((8, toks))] * len(stats),
-        out_specs=[pl.BlockSpec((BLK, toks), lambda j: (j, 0)), whole((8, toks))],
+        out_specs=[pl.BlockSpec((BLK, toks), lambda j: (jnp.maximum(j - 1, 0), 0)), whole((8, toks))],
         out_shape=[jax.ShapeDtypeStruct((vocab, toks), F32), jax.ShapeDtypeStruct((8, toks), F32)],
+        scratch_shapes=[pltpu.VMEM((BLK, toks), F32)],
         compiler_params=params(1),
         cost_estimate=pl.CostEstimate(
             flops=2 * vocab * dim * toks, bytes_accessed=vocab * dim * 2 + vocab * toks * 4,
@@ -150,11 +158,11 @@
     vocab, dim = wt.shape
     toks = z.shape[1]
     rows = toks // 2
-    steps = pl.cdiv(vocab, BLK)
+    steps = pl.cdiv(vocab, BACK_BLK)
     mixing = bool(pair)
-    in_specs = [whole((8, toks))] * 3 + [whole((8, 128)), pl.BlockSpec((BLK, toks), lambda j: (j, 0)),
-                                         pl.BlockSpec((BLK, dim), lambda j: (j, 0))]
-    out_specs = [pl.BlockSpec((BLK, toks), lambda j: (j, k)), ANY, ANY, whole((8, 128))]
+    in_specs = [whole((8, toks))] * 3 + [whole((8, 128)), pl.BlockSpec((BACK_BLK, toks), lambda j: (j, 0)),
+                                         pl.BlockSpec((BACK_BLK, dim), lambda j: (j, 0))]
+    out_specs = [pl.BlockSpec((BACK_BLK, toks), lambda j: (j, k)), ANY, ANY, whole((8, 128))]
     out_shape = [jax.ShapeDtypeStruct((vocab, 4 * toks), BF16), jax.ShapeDtypeStruct((rows, dim), F32),
                  jax.ShapeDtypeStruct((rows, dim), F32), jax.ShapeDtypeStruct((8, 128), F32)]
     if mixing:
@@ -166,7 +174,7 @@
         out_shape += [jax.ShapeDtypeStruct((rows // 2, dhalf), F32)] * 4
     args = [label, lse, scale, loss, z, wt, *pair, *shared]
     return pl.pallas_call(
-        functools.partial(back_body, k, mixing, BLK, vocab),
+        functools.partial(back_body, k, mixing, BACK_BLK, vocab),
         grid=(steps,),
         in_specs=in_specs + [ANY] * len(shared),
         out_specs=out_specs,

time: 469 us -> 465 us (level)
  transfers between devices with their start and end apart: 26 -> 26, of which waited for: 6 -> 6; matrix products, arithmetic and copies ran while one was open for 0% -> 0% of each run, Pallas kernels for 50% -> 49%
where the time goes in v3:
time: 465 us; the launch traced here: 457 us
  Pallas kernels  332 us (71%)
  waiting for transfers between devices  102 us (22%)
  starting transfers between devices  19 us (4%)
    pallas_call x4, Pallas kernels, back_call(): pl.pallas_call(functools.partial(back_body, k, mixing, BACK_BLK, vocab),...  111 us
    ppermute x26, waiting for transfers between devices, swap(): return lax.ppermute(v, 'vp', [(i, i ^ mask) for i in range(n)])  102 us
    pallas_call x4, Pallas kernels, fwd_call(): pl.pallas_call(functools.partial(fwd_body, k, len(parts), BLK), grid=(blo...  98.1 us
    pallas_call x1, Pallas kernels, weight_call(): pl.pallas_call(functools.partial(weight_body, len(parts)), grid=(dim // c...  81.3 us
    ppermute x26, starting transfers between devices, swap(): return lax.ppermute(v, 'vp', [(i, i ^ mask) for i in range(n)])  19 us
    pallas_call x2, Pallas kernels, small_call(): pl.pallas_call(body, in_specs=[vm] * len(args), out_specs=[vm] * len(outs...  14.8 us
  transfers between devices with their start and end apart: 26, of which 6 were waited for; matrix products, arithmetic and copies ran while one was open for 0% of the time, Pallas kernels for 49%

profile of v3, /device:TPU:0, one launch (start us, length us, event | category | flops | bytes accessed | tf_op | source)
XLA Modules:
  0.0 456.7 jit_solution(13205602011351302288)
XLA Ops:
  0.6 3.8 norm.1
  5.2 2.5 collective-permute-start
  7.7 1.5 collective-permute-start.9
  10.7 21.3 %collective-permute-done.refs_0_.refs_4_ = bf16[128,4096]{1,0:T(8,128)(2,1)} collective-permute-done((bf16[128,4096]{1,0:T(8,128)(2,1)}, bf16[128,4096]{1,0:T(8,128)(2,1)}, u32[]{:S(2)}, u32[]{:S(2)}) %collective-permute-start) | collective-permute-done | bytes 1048608 | tf_op jit(solution)/shard_map/ppermute | solution.py:456
  32.0 2.0 collective-permute-done.9.refs_1_.refs_5_
  34.0 1.5 collective-permute-start.1
  35.5 20.9 %collective-permute-done.2.refs_1_.refs_9_ = bf16[128,4096]{1,0:T(8,128)(2,1)} collective-permute-done((bf16[128,4096]{1,0:T(8,128)(2,1)}, bf16[128,4096]{1,0:T(8,128)(2,1)}, u32[]{:S(2)}, u32[]{:S(2)}) %collective-permute-start.2) | collective-permute-done | bytes 1048608 | tf_op jit(solution)/shard_map/ppermute | solution.py:456
  56.5 24.4 %fwd.4 = (f32[4016,512]{1,0:T(8,128)}, f32[8,512]{1,0:T(8,128)}) custom-call(s32[1]{0:T(128)} %bitcast.1.limit_ref, bf16[4016,4096]{1,0:T(8,128)(2,1)} %bitcast.10, bf16[128,4096]{1,0:T(8,128)(2,1)} %get-tuple-element.50.refs_0_, bf16[128,4096]{1,0:T(8,128)(2,1)} %get-tuple-element.51.refs_1_, bf16[128,4096]{1,0:T(8,128)(2,1)} %collective-permute-done.12.refs_2_, ...), custom_call_target="tpu_custom_call" | custom-call | flops 16844324864 | bytes 41123840 | tf_op jit(solution)/shard_map/fwd/pallas_call | solution.py:82
  82.0 24.5 %fwd.5 = (f32[4016,512]{1,0:T(8,128)}, f32[8,512]{1,0:T(8,128)}) custom-call(s32[1]{0:T(128)} %bitcast.1.limit_ref, bf16[4016,4096]{1,0:T(8,128)(2,1)} %bitcast.11, bf16[128,4096]{1,0:T(8,128)(2,1)} %collective-permute-done.refs_0_.refs_4_, bf16[128,4096]{1,0:T(8,128)(2,1)} %collective-permute-done.9.refs_1_.refs_5_, ...), custom_call_target="tpu_custom_call" | custom-call | flops 16844324864 | bytes 41123840 | tf_op jit(solution)/shard_map/fwd/pallas_call | solution.py:82
  106.5 24.7 %fwd.6 = (f32[4016,512]{1,0:T(8,128)}, f32[8,512]{1,0:T(8,128)}) custom-call(s32[1]{0:T(128)} %bitcast.1.limit_ref, bf16[4016,4096]{1,0:T(8,128)(2,1)} %bitcast.12, bf16[128,4096]{1,0:T(8,128)(2,1)} %collective-permute-done.6.refs_0_.refs_8_, bf16[128,4096]{1,0:T(8,128)(2,1)} %collective-permute-done.2.refs_1_.refs_9_, ...), custom_call_target="tpu_custom_call" | custom-call | flops 16844324864 | bytes 41123840 | tf_op jit(solution)/shard_map/fwd/pallas_call | solution.py:82
  131.2 24.5 %fwd.7 = (f32[4016,512]{1,0:T(8,128)}, f32[8,512]{1,0:T(8,128)}) custom-call(s32[1]{0:T(128)} %bitcast.1.limit_ref, bf16[4016,4096]{1,0:T(8,128)(2,1)} %bitcast.13, bf16[128,4096]{1,0:T(8,128)(2,1)} %collective-permute-done.1.refs_0_.refs_12_, bf16[128,4096]{1,0:T(8,128)(2,1)} %collective-permute-done.3.refs_1_.refs_13_, ...), custom_call_target="tpu_custom_call" | custom-call | flops 16844324864 | bytes 41123840 | tf_op jit(solution)/shard_map/fwd/pallas_call | solution.py:82
  155.7 7.8 %shard_map.84 = (s32[8,512]{1,0:T(8,128)}, f32[8,512]{1,0:T(8,128)}, f32[8,512]{1,0:T(8,128)}, f32[8,128]{1,0:T(8,128)}) custom-call(f32[8,512]{1,0:T(8,128)} %get-tuple-element.55.stat_ref, s32[2,128]{1,0:T(2,128)} %bitcast.21, f32[2,128]{1,0:T(2,128)} %bitcast.22), custom_call_target="tpu_custom_call" | custom-call | flops 4000 | bytes 4000000 | tf_op jit(solution)/shard_map/pallas_call | solution.py:344
  163.5 27.3 %back.4 = (bf16[4016,2048]{1,0:T(8,128)(2,1)}, f32[256,4096]{1,0:T(8,128)}, f32[256,4096]{1,0:T(8,128)}, f32[8,128]{1,0:T(8,128)}) custom-call(s32[8,512]{1,0:T(8,128)} %get-tuple-element.56.label_ref, f32[8,512]{1,0:T(8,128)} %get-tuple-element.57.lse_ref, f32[8,512]{1,0:T(8,128)} %get-tuple-element.58.scale_ref, f32[8,128]{1,0:T(8,128)} %get-tuple-element.59.loss_ref, ...), custom_call_target="tpu_custom_call" | custom-call | flops 16844324864 | bytes 45236224 | tf_op jit(solution)/shard_map/back/pallas_call | solution.py:176
  190.8 27.4 %back.5 = (bf16[4016,2048]{1,0:T(8,128)(2,1)}, f32[256,4096]{1,0:T(8,128)}, f32[256,4096]{1,0:T(8,128)}, f32[8,128]{1,0:T(8,128)}) custom-call(s32[8,512]{1,0:T(8,128)} %get-tuple-element.56.label_ref, f32[8,512]{1,0:T(8,128)} %get-tuple-element.57.lse_ref, f32[8,512]{1,0:T(8,128)} %get-tuple-element.58.scale_ref, ...), custom_call_target="tpu_custom_call", output_to_operand_aliasing={{0}: (6, {})} | custom-call | flops 16844324864 | bytes 45236224 | tf_op jit(solution)/shard_map/back/pallas_call | solution.py:176
  218.7 27.6 %back.6 = (bf16[4016,2048]{1,0:T(8,128)(2,1)}, f32[256,4096]{1,0:T(8,128)}, f32[256,4096]{1,0:T(8,128)}, f32[8,128]{1,0:T(8,128)}) custom-call(s32[8,512]{1,0:T(8,128)} %get-tuple-element.56.label_ref, f32[8,512]{1,0:T(8,128)} %get-tuple-element.57.lse_ref, f32[8,512]{1,0:T(8,128)} %get-tuple-element.58.scale_ref, ...), custom_call_target="tpu_custom_call", output_to_operand_aliasing={{0}: (6, {})} | custom-call | flops 16844324864 | bytes 45236224 | tf_op jit(solution)/shard_map/back/pallas_call | solution.py:176
  246.4 29.3 %back.7 = (bf16[4016,2048]{1,0:T(8,128)(2,1)}, f32[256,4096]{1,0:T(8,128)}, f32[256,4096]{1,0:T(8,128)}, f32[8,128]{1,0:T(8,128)}, f32[128,2048]{1,0:T(8,128)}, ...) custom-call(s32[8,512]{1,0:T(8,128)} %get-tuple-element.56.label_ref, ...), custom_call_target="tpu_custom_call", output_to_operand_aliasing={{0}: (8, {})} | custom-call | flops 16844324864 | bytes 45236224 | tf_op jit(solution)/shard_map/back/pallas_call | solution.py:176
  276.1 5.7 %mix.1 = (f32[256,2048]{1,0:T(8,128)}, f32[256,2048]{1,0:T(8,128)}) custom-call(f32[256,4096]{1,0:T(8,128)} %get-tuple-element.81.keep_ref, f32[256,4096]{1,0:T(8,128)} %collective-permute-done.18.got_ref), custom_call_target="tpu_custom_call" | custom-call | flops 1048576 | bytes 12582912 | tf_op jit(solution)/shard_map/mix/pallas_call | solution.py:366
  285.9 44.8 %collective-permute-done.19.xa_ref.xb_ref = f32[256,2048]{1,0:T(8,128)} collective-permute-done((f32[256,2048]{1,0:T(8,128)}, f32[256,2048]{1,0:T(8,128)}, u32[]{:S(2)}, u32[]{:S(2)}) %collective-permute-start.19) | collective-permute-done | bytes 2097184 | tf_op jit(solution)/shard_map/ppermute | solution.py:456
  330.7 1.5 collective-permute-done.20.ya_ref.yb_ref
  332.2 7.8 %second.1 = (f32[128,2048]{1,0:T(8,128)}, f32[128,2048]{1,0:T(8,128)}, f32[2,128,2048]{2,1,0:T(8,128)}, f32[2,128,2048]{2,1,0:T(8,128)}) custom-call(f32[256,4096]{1,0:T(8,128)} %get-tuple-element.77.keep2_ref.keep4_ref, f32[256,4096]{1,0:T(8,128)} %get-tuple-element.77.keep2_ref.keep4_ref, f32[256,4096]{1,0:T(8,128)} %collective-permute-done.17.got2_ref.got4_ref, ...), custom_call_target="tpu_custom_call" | custom-call | flops 2097152 | bytes 20971520 | tf_op jit(solution)/shard_map/second/pallas_call | solution.py:397
  342.0 11.2 %collective-permute-done.16.x2a_ref = f32[128,2048]{1,0:T(8,128)} collective-permute-done((f32[128,2048]{1,0:T(8,128)}, f32[128,2048]{1,0:T(8,128)}, u32[]{:S(2)}, u32[]{:S(2)}) %collective-permute-start.16) | collective-permute-done | bytes 1048608 | tf_op jit(solution)/shard_map/ppermute | solution.py:456
  356.1 81.3 %dweight.1 = (f32[4016,4096]{1,0:T(8,128)}, f32[256,4096]{1,0:T(8,128)}) custom-call(bf16[4016,2048]{1,0:T(8,128)(2,1)} %get-tuple-element.72.dz_ref, f32[256,4096]{1,0:T(8,128)} %get-tuple-element.73.keep_ref, f32[256,4096]{1,0:T(8,128)} %collective-permute-done.15.got_ref, bf16[128,4096]{1,0:T(8,128)(2,1)} %get-tuple-element.50.refs_0_, ...), custom_call_target="tpu_custom_call" | custom-call | flops 67377299456 | bytes 98697216 | tf_op jit(solution)/shard_map/dweight/pallas_call | solution.py:209
  437.5 8.9 %last.1 = (bf16[256,4096]{1,0:T(8,128)(2,1)}, f32[8,512]{1,0:T(8,128)}) custom-call(bf16[256,4096]{1,0:T(8,128)(2,1)} %hid_ref.1, f32[1,4096]{1,0:T(1,128)} %bitcast.19, f32[256,4096]{1,0:T(8,128)} %get-tuple-element.75.q_ref, f32[128,2048]{1,0:T(8,128)} %collective-permute-done.16.x2a_ref, f32[128,2048]{1,0:T(8,128)} %collective-permute-done.21.x2b_ref, ...), custom_call_target="tpu_custom_call" | custom-call | flops 20971520 | bytes 20971520 | tf_op jit(solution)/shard_map/last/pallas_call | solution.py:440
  446.3 7.1 %shard_map.85 = (f32[32,128]{1,0:T(8,128)}, f32[1,1]{1,0:T(1,128)}) custom-call(f32[8,512]{1,0:T(8,128)} %get-tuple-element.90.gain_ref, f32[8,128]{1,0:T(8,128)} %get-tuple-element.91.loss_ref), custom_call_target="tpu_custom_call" | custom-call | flops 4000 | bytes 4000000 | tf_op jit(solution)/shard_map/pallas_call | solution.py:344
  (44 shorter events, 14.9 us)
Async XLA Ops:
  5.2 26.8 %collective-permute-start = (bf16[128,4096]{1,0:T(8,128)(2,1)}, bf16[128,4096]{1,0:T(8,128)(2,1)}, u32[]{:S(2)}, u32[]{:S(2)}) collective-permute-start(bf16[128,4096]{1,0:T(8,128)(2,1)} %get-tuple-element.50.refs_0_), channel_id=1, source_target_pairs={{0,2},{1,3},{2,0},{3,1},{4,6},{5,7},{6,4},{7,5},{8,10},{9,11},{10,... | collective-permute-start | bytes 3145736 | tf_op jit(solution)/shard_map/ppermute | solution.py:456
  7.7 26.3 %collective-permute-start.9 = (bf16[128,4096]{1,0:T(8,128)(2,1)}, bf16[128,4096]{1,0:T(8,128)(2,1)}, u32[]{:S(2)}, u32[]{:S(2)}) collective-permute-start(bf16[128,4096]{1,0:T(8,128)(2,1)} %get-tuple-element.50.refs_0_), channel_id=1, source_target_pairs={{0,4},{1,5},{2,6},{3,7},{4,0},{5,1},{6,2},{7,3},{8,12},{9,13},{10,... | collective-permute-start | bytes 3145736 | tf_op jit(solution)/shard_map/ppermute | solution.py:456
  9.2 26.4 %collective-permute-start.13 = (bf16[128,4096]{1,0:T(8,128)(2,1)}, bf16[128,4096]{1,0:T(8,128)(2,1)}, u32[]{:S(2)}, u32[]{:S(2)}) collective-permute-start(bf16[128,4096]{1,0:T(8,128)(2,1)} %get-tuple-element.51.refs_1_), channel_id=1, source_target_pairs={{0,1},{1,0},{2,3},{3,2},{4,5},{5,4},{6,7},{7,6},{8,9},{9,8},{10,11... | collective-permute-start | bytes 3145736 | tf_op jit(solution)/shard_map/ppermute | solution.py:456
  9.2 47.3 %collective-permute-start.2 = (bf16[128,4096]{1,0:T(8,128)(2,1)}, bf16[128,4096]{1,0:T(8,128)(2,1)}, u32[]{:S(2)}, u32[]{:S(2)}) collective-permute-start(bf16[128,4096]{1,0:T(8,128)(2,1)} %get-tuple-element.51.refs_1_), channel_id=1, source_target_pairs={{0,4},{1,5},{2,6},{3,7},{4,0},{5,1},{6,2},{7,3},{8,12},{9,13},{10,... | collective-permute-start | bytes 3145736 | tf_op jit(solution)/shard_map/ppermute | solution.py:456
  9.7 71.3 %collective-permute-start.6 = (bf16[128,4096]{1,0:T(8,128)(2,1)}, bf16[128,4096]{1,0:T(8,128)(2,1)}, u32[]{:S(2)}, u32[]{:S(2)}) collective-permute-start(bf16[128,4096]{1,0:T(8,128)(2,1)} %get-tuple-element.51.refs_1_), channel_id=1, source_target_pairs={{0,2},{1,3},{2,0},{3,1},{4,6},{5,7},{6,4},{7,5},{8,10},{9,11},{10,... | collective-permute-start | bytes 3145736 | tf_op jit(solution)/shard_map/ppermute | solution.py:456
  32.0 50.0 %collective-permute-start.10 = (bf16[128,4096]{1,0:T(8,128)(2,1)}, bf16[128,4096]{1,0:T(8,128)(2,1)}, u32[]{:S(2)}, u32[]{:S(2)}) collective-permute-start(bf16[128,4096]{1,0:T(8,128)(2,1)} %collective-permute-done.refs_0_.refs_4_), channel_id=1, source_target_pairs={{0,1},{1,0},{2,3},{3,2},{4,5},{5,4},{6,7},{7,6},{8,9},{9,8},{10,11... | collective-permute-start | bytes 3145736 | tf_op jit(solution)/shard_map/ppermute | solution.py:456
  34.0 47.5 %collective-permute-start.1 = (bf16[128,4096]{1,0:T(8,128)(2,1)}, bf16[128,4096]{1,0:T(8,128)(2,1)}, u32[]{:S(2)}, u32[]{:S(2)}) collective-permute-start(bf16[128,4096]{1,0:T(8,128)(2,1)} %collective-permute-done.refs_0_.refs_4_), channel_id=1, source_target_pairs={{0,4},{1,5},{2,6},{3,7},{4,0},{5,1},{6,2},{7,3},{8,12},{9,13},{10,... | collective-permute-start | bytes 3145736 | tf_op jit(solution)/shard_map/ppermute | solution.py:456
  35.5 45.5 %collective-permute-start.11 = (bf16[128,4096]{1,0:T(8,128)(2,1)}, bf16[128,4096]{1,0:T(8,128)(2,1)}, u32[]{:S(2)}, u32[]{:S(2)}) collective-permute-start(bf16[128,4096]{1,0:T(8,128)(2,1)} %collective-permute-done.9.refs_1_.refs_5_), channel_id=1, source_target_pairs={{0,1},{1,0},{2,3},{3,2},{4,5},{5,4},{6,7},{7,6},{8,9},{9,8},{10,11... | collective-permute-start | bytes 3145736 | tf_op jit(solution)/shard_map/ppermute | solution.py:456
  81.0 25.5 %collective-permute-start.8 = (bf16[128,4096]{1,0:T(8,128)(2,1)}, bf16[128,4096]{1,0:T(8,128)(2,1)}, u32[]{:S(2)}, u32[]{:S(2)}) collective-permute-start(bf16[128,4096]{1,0:T(8,128)(2,1)} %collective-permute-done.2.refs_1_.refs_9_), channel_id=1, source_target_pairs={{0,1},{1,0},{2,3},{3,2},{4,5},{5,4},{6,7},{7,6},{8,9},{9,8},{10,11... | collective-permute-start | bytes 3145736 | tf_op jit(solution)/shard_map/ppermute | solution.py:456
  81.0 25.5 %collective-permute-start.7 = (bf16[128,4096]{1,0:T(8,128)(2,1)}, bf16[128,4096]{1,0:T(8,128)(2,1)}, u32[]{:S(2)}, u32[]{:S(2)}) collective-permute-start(bf16[128,4096]{1,0:T(8,128)(2,1)} %collective-permute-done.6.refs_0_.refs_8_), channel_id=1, source_target_pairs={{0,1},{1,0},{2,3},{3,2},{4,5},{5,4},{6,7},{7,6},{8,9},{9,8},{10,11... | collective-permute-start | bytes 3145736 | tf_op jit(solution)/shard_map/ppermute | solution.py:456
  81.5 49.7 %collective-permute-start.4 = (bf16[128,4096]{1,0:T(8,128)(2,1)}, bf16[128,4096]{1,0:T(8,128)(2,1)}, u32[]{:S(2)}, u32[]{:S(2)}) collective-permute-start(bf16[128,4096]{1,0:T(8,128)(2,1)} %collective-permute-done.1.refs_0_.refs_12_), channel_id=1, source_target_pairs={{0,1},{1,0},{2,3},{3,2},{4,5},{5,4},{6,7},{7,6},{8,9},{9,8},{10,11... | collective-permute-start | bytes 3145736 | tf_op jit(solution)/shard_map/ppermute | solution.py:456
  81.6 49.6 %collective-permute-start.5 = (bf16[128,4096]{1,0:T(8,128)(2,1)}, bf16[128,4096]{1,0:T(8,128)(2,1)}, u32[]{:S(2)}, u32[]{:S(2)}) collective-permute-start(bf16[128,4096]{1,0:T(8,128)(2,1)} %collective-permute-done.3.refs_1_.refs_13_), channel_id=1, source_target_pairs={{0,1},{1,0},{2,3},{3,2},{4,5},{5,4},{6,7},{7,6},{8,9},{9,8},{10,11... | collective-permute-start | bytes 3145736 | tf_op jit(solution)/shard_map/ppermute | solution.py:456
  218.1 28.3 %collective-permute-start.14 = (f32[256,4096]{1,0:T(8,128)}, f32[256,4096]{1,0:T(8,128)}, u32[]{:S(2)}, u32[]{:S(2)}) collective-permute-start(f32[256,4096]{1,0:T(8,128)} %get-tuple-element.70), channel_id=1, source_target_pairs={{0,1},{1,0},{2,3},{3,2},{4,5},{5,4},{6,7},{7,6},{8,9},{9,8},{10,11... | collective-permute-start | bytes 12582920 | tf_op jit(solution)/shard_map/ppermute | solution.py:456
  218.3 57.8 %collective-permute-start.18 = (f32[256,4096]{1,0:T(8,128)}, f32[256,4096]{1,0:T(8,128)}, u32[]{:S(2)}, u32[]{:S(2)}) collective-permute-start(f32[256,4096]{1,0:T(8,128)} %get-tuple-element.82), channel_id=1, source_target_pairs={{0,1},{1,0},{2,3},{3,2},{4,5},{5,4},{6,7},{7,6},{8,9},{9,8},{10,11... | collective-permute-start | bytes 12582920 | tf_op jit(solution)/shard_map/ppermute | solution.py:456
  246.3 39.1 %collective-permute-start.17 = (f32[256,4096]{1,0:T(8,128)}, f32[256,4096]{1,0:T(8,128)}, u32[]{:S(2)}, u32[]{:S(2)}) collective-permute-start(f32[256,4096]{1,0:T(8,128)} %get-tuple-element.78), channel_id=1, source_target_pairs={{0,1},{1,0},{2,3},{3,2},{4,5},{5,4},{6,7},{7,6},{8,9},{9,8},{10,11... | collective-permute-start | bytes 12582920 | tf_op jit(solution)/shard_map/ppermute | solution.py:456
  275.7 79.0 %collective-permute-start.15 = (f32[256,4096]{1,0:T(8,128)}, f32[256,4096]{1,0:T(8,128)}, u32[]{:S(2)}, u32[]{:S(2)}) collective-permute-start(f32[256,4096]{1,0:T(8,128)} %get-tuple-element.74), channel_id=1, source_target_pairs={{0,1},{1,0},{2,3},{3,2},{4,5},{5,4},{6,7},{7,6},{8,9},{9,8},{10,11... | collective-permute-start | bytes 12582920 | tf_op jit(solution)/shard_map/ppermute | solution.py:456
  281.9 48.8 %collective-permute-start.19 = (f32[256,2048]{1,0:T(8,128)}, f32[256,2048]{1,0:T(8,128)}, u32[]{:S(2)}, u32[]{:S(2)}) collective-permute-start(f32[256,2048]{1,0:T(8,128)} %get-tuple-element.83), channel_id=1, source_target_pairs={{0,2},{1,3},{2,0},{3,1},{4,6},{5,7},{6,4},{7,5},{8,10},{9,11},{10,... | collective-permute-start | bytes 6291464 | tf_op jit(solution)/shard_map/ppermute | solution.py:456
  283.4 48.8 %collective-permute-start.20 = (f32[256,2048]{1,0:T(8,128)}, f32[256,2048]{1,0:T(8,128)}, u32[]{:S(2)}, u32[]{:S(2)}) collective-permute-start(f32[256,2048]{1,0:T(8,128)} %get-tuple-element.84), channel_id=1, source_target_pairs={{0,4},{1,5},{2,6},{3,7},{4,0},{5,1},{6,2},{7,3},{8,12},{9,13},{10,... | collective-permute-start | bytes 6291464 | tf_op jit(solution)/shard_map/ppermute | solution.py:456
  284.8 68.3 %collective-permute-start.16 = (f32[128,2048]{1,0:T(8,128)}, f32[128,2048]{1,0:T(8,128)}, u32[]{:S(2)}, u32[]{:S(2)}) collective-permute-start(f32[128,2048]{1,0:T(8,128)} %get-tuple-element.76), channel_id=1, source_target_pairs={{0,2},{1,3},{2,0},{3,1},{4,6},{5,7},{6,4},{7,5},{8,10},{9,11},{10,... | collective-permute-start | bytes 3145736 | tf_op jit(solution)/shard_map/ppermute | solution.py:456
  285.4 152.0 %collective-permute-start.23 = (f32[128,2048]{1,0:T(8,128)}, f32[128,2048]{1,0:T(8,128)}, u32[]{:S(2)}, u32[]{:S(2)}) collective-permute-start(f32[128,2048]{1,0:T(8,128)} %get-tuple-element.87), channel_id=1, source_target_pairs={{0,4},{1,5},{2,6},{3,7},{4,0},{5,1},{6,2},{7,3},{8,12},{9,13},{10,... | collective-permute-start | bytes 3145736 | tf_op jit(solution)/shard_map/ppermute | solution.py:456
  339.9 97.5 %collective-permute-start.21 = (f32[128,2048]{1,0:T(8,128)}, f32[128,2048]{1,0:T(8,128)}, u32[]{:S(2)}, u32[]{:S(2)}) collective-permute-start(f32[128,2048]{1,0:T(8,128)} %get-tuple-element.85), channel_id=1, source_target_pairs={{0,2},{1,3},{2,0},{3,1},{4,6},{5,7},{6,4},{7,5},{8,10},{9,11},{10,... | collective-permute-start | bytes 3145736 | tf_op jit(solution)/shard_map/ppermute | solution.py:456
  340.5 96.9 %collective-permute-start.24 = (f32[128,2048]{1,0:T(8,128)}, f32[128,2048]{1,0:T(8,128)}, u32[]{:S(2)}, u32[]{:S(2)}) collective-permute-start(f32[128,2048]{1,0:T(8,128)} %get-tuple-element.88), channel_id=1, source_target_pairs={{0,4},{1,5},{2,6},{3,7},{4,0},{5,1},{6,2},{7,3},{8,12},{9,13},{10,... | collective-permute-start | bytes 3145736 | tf_op jit(solution)/shard_map/ppermute | solution.py:456
  353.2 84.3 %collective-permute-start.22 = (f32[2,128,2048]{2,1,0:T(8,128)}, f32[2,128,2048]{2,1,0:T(8,128)}, u32[]{:S(2)}, u32[]{:S(2)}) collective-permute-start(f32[2,128,2048]{2,1,0:T(8,128)} %get-tuple-element.86), channel_id=1, source_target_pairs={{0,4},{1,5},{2,6},{3,7},{4,0},{5,1},{6,2},{7,3},{8,12},{9,13},{10,... | collective-permute-start | bytes 6291464 | tf_op jit(solution)/shard_map/ppermute | solution.py:456
  354.6 82.8 %collective-permute-start.25 = (f32[2,128,2048]{2,1,0:T(8,128)}, f32[2,128,2048]{2,1,0:T(8,128)}, u32[]{:S(2)}, u32[]{:S(2)}) collective-permute-start(f32[2,128,2048]{2,1,0:T(8,128)} %get-tuple-element.89), channel_id=1, source_target_pairs={{0,2},{1,3},{2,0},{3,1},{4,6},{5,7},{6,4},{7,5},{8,10},{9,11},{10,... | collective-permute-start | bytes 6291464 | tf_op jit(solution)/shard_map/ppermute | solution.py:456
  (2 other events, 30.3 us)

commit v4 on v3

--- a/solution.py
+++ b/solution.py
@@ -112,12 +112,30 @@
 
 
 def back_body(k, mixing, blk, vocab, label_ref, lse_ref, scale_ref, loss_ref, z_ref, wt_ref, *refs):
-    dz_ref, keep_ref, send_ref, lost_ref = refs[-10:-6] if mixing else refs[-6:-2]
-    acc_ref, sem = refs[-2:]
+    dz_ref, keep_ref, send_ref, lost_ref = refs[-12:-8] if mixing else refs[-8:-4]
+    acc_ref, w_ref, sem, w_sem = refs[-4:]
     step, steps = pl.program_id(0), pl.num_programs(0)
     tail = vocab - (vocab // blk) * blk or blk
     rows, dim = keep_ref.shape
     row = slice(k, k + 1)
+    wide = dim // 2
+
+    def fetch(block, size):
+        slot = lax.rem(block, 2)
+        at = pl.ds(pl.multiple_of(block * blk, blk), size)
+        return [
+            pltpu.make_async_copy(
+                wt_ref.at[at, h * wide:(h + 1) * wide], w_ref.at[slot, 0:size, h * wide:(h + 1) * wide], w_sem.at[slot, h])
+            for h in range(2)
+        ]
+
+    def begin(block, size):
+        for c in fetch(block, size):
+            c.start()
+
+    pl.when(step == 0)(lambda: begin(step, blk))
+    pl.when(step + 1 < steps - 1)(lambda: begin(step + 1, blk))
+    pl.when(step + 1 == steps - 1)(lambda: begin(step + 1, tail))
 
     @pl.when(step == 0)
     def _():
@@ -125,9 +143,11 @@
         lost_ref[...] = loss_ref[...]
 
     if mixing:
-        mix(step < steps // 2, refs[0], refs[1], refs[-6:-2])
+        mix(step < steps // 2, refs[0], refs[1], refs[-8:-4])
 
     def run(size, leave):
+        arriving = fetch(step, size)
+        arriving[0].wait()
         z = z_ref[:size]
         col = step * blk + lax.broadcasted_iota(jnp.int32, z.shape, 0)
         hit = col == label_ref[row]
@@ -135,13 +155,15 @@
         dz = ((jnp.exp(z - lse_ref[row]) - jnp.where(hit, 1.0, 0.0)) * scale).astype(BF16)
         dz_ref[:size] = dz
         lost = jnp.sum(jnp.where(hit, z, 0.0), axis=0, keepdims=True) * scale
-        wide = lost_ref.shape[1]
-        lost_ref[0:1] = lost_ref[0:1] - sum(lost[:, i:i + wide] for i in range(0, lost.shape[1], wide))
-        copies = []
+        part = lost_ref.shape[1]
+        lost_ref[0:1] = lost_ref[0:1] - sum(lost[:, i:i + part] for i in range(0, lost.shape[1], part))
+        copies, slot = [], lax.rem(step, 2)
         for t in range(dim // TILE):
             cols = slice(t * TILE, (t + 1) * TILE)
+            if t * TILE == wide:
+                arriving[1].wait()
             acc_ref[:, cols] += lax.dot_general(
-                dz, wt_ref[:size, cols], (((0,), (0,)), ((), ())), preferred_element_type=F32)
+                dz, w_ref[slot, :size, cols], (((0,), (0,)), ((), ())), preferred_element_type=F32)
             if leave:
                 for h, out in enumerate((keep_ref, send_ref)):
                     copies.append(pltpu.make_async_copy(
@@ -161,7 +183,7 @@
     steps = pl.cdiv(vocab, BACK_BLK)
     mixing = bool(pair)
     in_specs = [whole((8, toks))] * 3 + [whole((8, 128)), pl.BlockSpec((BACK_BLK, toks), lambda j: (j, 0)),
-                                         pl.BlockSpec((BACK_BLK, dim), lambda j: (j, 0))]
+                                         ANY]
     out_specs = [pl.BlockSpec((BACK_BLK, toks), lambda j: (j, k)), ANY, ANY, whole((8, 128))]
     out_shape = [jax.ShapeDtypeStruct((vocab, 4 * toks), BF16), jax.ShapeDtypeStruct((rows, dim), F32),
                  jax.ShapeDtypeStruct((rows, dim), F32), jax.ShapeDtypeStruct((8, 128), F32)]
@@ -180,7 +202,8 @@
         out_specs=out_specs,
         out_shape=out_shape,
         input_output_aliases={len(args) - 1: 0} if shared else {},
-        scratch_shapes=[pltpu.VMEM((toks, dim), F32), pltpu.SemaphoreType.DMA((2 * dim // TILE,))],
+        scratch_shapes=[pltpu.VMEM((toks, dim), F32), pltpu.VMEM((2, BACK_BLK, dim), BF16),
+                        pltpu.SemaphoreType.DMA((2 * dim // TILE,)), pltpu.SemaphoreType.DMA((2, 2))],
         compiler_params=params(1),
         cost_estimate=pl.CostEstimate(
             flops=2 * vocab * dim * toks, bytes_accessed=vocab * dim * 2 + vocab * toks * 6,

time: 465 us -> 465 us (level)
  no operation moved by 1% of the time
where the time goes in v4:
time: 465 us; the launch traced here: 457 us
  Pallas kernels  332 us (71%)
  waiting for transfers between devices  102 us (22%)
  starting transfers between devices  19 us (4%)
    pallas_call x4, Pallas kernels, back_call(): pl.pallas_call(functools.partial(back_body, k, mixing, BACK_BLK, vocab),...  112 us
    ppermute x26, waiting for transfers between devices, swap(): return lax.ppermute(v, 'vp', [(i, i ^ mask) for i in range(n)])  102 us
    pallas_call x4, Pallas kernels, fwd_call(): pl.pallas_call(functools.partial(fwd_body, k, len(parts), BLK), grid=(blo...  98.1 us
    pallas_call x1, Pallas kernels, weight_call(): pl.pallas_call(functools.partial(weight_body, len(parts)), grid=(dim // c...  81.3 us
    ppermute x26, starting transfers between devices, swap(): return lax.ppermute(v, 'vp', [(i, i ^ mask) for i in range(n)])  19 us
    pallas_call x2, Pallas kernels, small_call(): pl.pallas_call(body, in_specs=[vm] * len(args), out_specs=[vm] * len(outs...  14.8 us
  transfers between devices with their start and end apart: 26, of which 6 were waited for; matrix products, arithmetic and copies ran while one was open for 0% of the time, Pallas kernels for 49%

profile of v4, /device:TPU:0, one launch (start us, length us, event | category | flops | bytes accessed | tf_op | source)
XLA Modules:
  0.0 457.3 jit_solution(15747455953559308777)
XLA Ops:
  0.6 3.8 norm.1
  5.2 2.5 collective-permute-start
  10.7 21.3 %collective-permute-done.refs_0_.refs_4_ = bf16[128,4096]{1,0:T(8,128)(2,1)} collective-permute-done((bf16[128,4096]{1,0:T(8,128)(2,1)}, bf16[128,4096]{1,0:T(8,128)(2,1)}, u32[]{:S(2)}, u32[]{:S(2)}) %collective-permute-start) | collective-permute-done | bytes 1048608 | tf_op jit(solution)/shard_map/ppermute | solution.py:479
  32.0 2.0 collective-permute-done.9.refs_1_.refs_5_
  35.5 20.9 %collective-permute-done.2.refs_1_.refs_9_ = bf16[128,4096]{1,0:T(8,128)(2,1)} collective-permute-done((bf16[128,4096]{1,0:T(8,128)(2,1)}, bf16[128,4096]{1,0:T(8,128)(2,1)}, u32[]{:S(2)}, u32[]{:S(2)}) %collective-permute-start.2) | collective-permute-done | bytes 1048608 | tf_op jit(solution)/shard_map/ppermute | solution.py:479
  56.5 24.4 %fwd.4 = (f32[4016,512]{1,0:T(8,128)}, f32[8,512]{1,0:T(8,128)}) custom-call(s32[1]{0:T(128)} %bitcast.1.limit_ref, bf16[4016,4096]{1,0:T(8,128)(2,1)} %bitcast.10, bf16[128,4096]{1,0:T(8,128)(2,1)} %get-tuple-element.50.refs_0_, bf16[128,4096]{1,0:T(8,128)(2,1)} %get-tuple-element.51.refs_1_, bf16[128,4096]{1,0:T(8,128)(2,1)} %collective-permute-done.12.refs_2_, ...), custom_call_target="tpu_custom_call" | custom-call | flops 16844324864 | bytes 41123840 | tf_op jit(solution)/shard_map/fwd/pallas_call | solution.py:82
  82.0 24.5 %fwd.5 = (f32[4016,512]{1,0:T(8,128)}, f32[8,512]{1,0:T(8,128)}) custom-call(s32[1]{0:T(128)} %bitcast.1.limit_ref, bf16[4016,4096]{1,0:T(8,128)(2,1)} %bitcast.11, bf16[128,4096]{1,0:T(8,128)(2,1)} %collective-permute-done.refs_0_.refs_4_, bf16[128,4096]{1,0:T(8,128)(2,1)} %collective-permute-done.9.refs_1_.refs_5_, ...), custom_call_target="tpu_custom_call" | custom-call | flops 16844324864 | bytes 41123840 | tf_op jit(solution)/shard_map/fwd/pallas_call | solution.py:82
  106.5 24.7 %fwd.6 = (f32[4016,512]{1,0:T(8,128)}, f32[8,512]{1,0:T(8,128)}) custom-call(s32[1]{0:T(128)} %bitcast.1.limit_ref, bf16[4016,4096]{1,0:T(8,128)(2,1)} %bitcast.12, bf16[128,4096]{1,0:T(8,128)(2,1)} %collective-permute-done.6.refs_0_.refs_8_, bf16[128,4096]{1,0:T(8,128)(2,1)} %collective-permute-done.2.refs_1_.refs_9_, ...), custom_call_target="tpu_custom_call" | custom-call | flops 16844324864 | bytes 41123840 | tf_op jit(solution)/shard_map/fwd/pallas_call | solution.py:82
  131.2 24.5 %fwd.7 = (f32[4016,512]{1,0:T(8,128)}, f32[8,512]{1,0:T(8,128)}) custom-call(s32[1]{0:T(128)} %bitcast.1.limit_ref, bf16[4016,4096]{1,0:T(8,128)(2,1)} %bitcast.13, bf16[128,4096]{1,0:T(8,128)(2,1)} %collective-permute-done.1.refs_0_.refs_12_, bf16[128,4096]{1,0:T(8,128)(2,1)} %collective-permute-done.3.refs_1_.refs_13_, ...), custom_call_target="tpu_custom_call" | custom-call | flops 16844324864 | bytes 41123840 | tf_op jit(solution)/shard_map/fwd/pallas_call | solution.py:82
  155.7 7.8 %shard_map.84 = (s32[8,512]{1,0:T(8,128)}, f32[8,512]{1,0:T(8,128)}, f32[8,512]{1,0:T(8,128)}, f32[8,128]{1,0:T(8,128)}) custom-call(f32[8,512]{1,0:T(8,128)} %get-tuple-element.55.stat_ref, s32[2,128]{1,0:T(2,128)} %bitcast.21, f32[2,128]{1,0:T(2,128)} %bitcast.22), custom_call_target="tpu_custom_call" | custom-call | flops 4000 | bytes 4000000 | tf_op jit(solution)/shard_map/pallas_call | solution.py:367
  163.5 27.3 %back.4 = (bf16[4016,2048]{1,0:T(8,128)(2,1)}, f32[256,4096]{1,0:T(8,128)}, f32[256,4096]{1,0:T(8,128)}, f32[8,128]{1,0:T(8,128)}) custom-call(s32[8,512]{1,0:T(8,128)} %get-tuple-element.56.label_ref, f32[8,512]{1,0:T(8,128)} %get-tuple-element.57.lse_ref, f32[8,512]{1,0:T(8,128)} %get-tuple-element.58.scale_ref, f32[8,128]{1,0:T(8,128)} %get-tuple-element.59.loss_ref, ...), custom_call_target="tpu_custom_call" | custom-call | flops 16844324864 | bytes 45236224 | tf_op jit(solution)/shard_map/back/pallas_call | solution.py:198
  190.8 27.4 %back.5 = (bf16[4016,2048]{1,0:T(8,128)(2,1)}, f32[256,4096]{1,0:T(8,128)}, f32[256,4096]{1,0:T(8,128)}, f32[8,128]{1,0:T(8,128)}) custom-call(s32[8,512]{1,0:T(8,128)} %get-tuple-element.56.label_ref, f32[8,512]{1,0:T(8,128)} %get-tuple-element.57.lse_ref, f32[8,512]{1,0:T(8,128)} %get-tuple-element.58.scale_ref, ...), custom_call_target="tpu_custom_call", output_to_operand_aliasing={{0}: (6, {})} | custom-call | flops 16844324864 | bytes 45236224 | tf_op jit(solution)/shard_map/back/pallas_call | solution.py:198
  218.8 27.6 %back.6 = (bf16[4016,2048]{1,0:T(8,128)(2,1)}, f32[256,4096]{1,0:T(8,128)}, f32[256,4096]{1,0:T(8,128)}, f32[8,128]{1,0:T(8,128)}) custom-call(s32[8,512]{1,0:T(8,128)} %get-tuple-element.56.label_ref, f32[8,512]{1,0:T(8,128)} %get-tuple-element.57.lse_ref, f32[8,512]{1,0:T(8,128)} %get-tuple-element.58.scale_ref, ...), custom_call_target="tpu_custom_call", output_to_operand_aliasing={{0}: (6, {})} | custom-call | flops 16844324864 | bytes 45236224 | tf_op jit(solution)/shard_map/back/pallas_call | solution.py:198
  246.6 29.6 %back.7 = (bf16[4016,2048]{1,0:T(8,128)(2,1)}, f32[256,4096]{1,0:T(8,128)}, f32[256,4096]{1,0:T(8,128)}, f32[8,128]{1,0:T(8,128)}, f32[128,2048]{1,0:T(8,128)}, ...) custom-call(s32[8,512]{1,0:T(8,128)} %get-tuple-element.56.label_ref, ...), custom_call_target="tpu_custom_call", output_to_operand_aliasing={{0}: (8, {})} | custom-call | flops 16844324864 | bytes 45236224 | tf_op jit(solution)/shard_map/back/pallas_call | solution.py:198
  276.7 5.7 %mix.1 = (f32[256,2048]{1,0:T(8,128)}, f32[256,2048]{1,0:T(8,128)}) custom-call(f32[256,4096]{1,0:T(8,128)} %get-tuple-element.81.keep_ref, f32[256,4096]{1,0:T(8,128)} %collective-permute-done.18.got_ref), custom_call_target="tpu_custom_call" | custom-call | flops 1048576 | bytes 12582912 | tf_op jit(solution)/shard_map/mix/pallas_call | solution.py:389
  282.4 1.5 collective-permute-start.19
  286.5 44.8 %collective-permute-done.19.xa_ref.xb_ref = f32[256,2048]{1,0:T(8,128)} collective-permute-done((f32[256,2048]{1,0:T(8,128)}, f32[256,2048]{1,0:T(8,128)}, u32[]{:S(2)}, u32[]{:S(2)}) %collective-permute-start.19) | collective-permute-done | bytes 2097184 | tf_op jit(solution)/shard_map/ppermute | solution.py:479
  331.2 1.5 collective-permute-done.20.ya_ref.yb_ref
  332.8 7.8 %second.1 = (f32[128,2048]{1,0:T(8,128)}, f32[128,2048]{1,0:T(8,128)}, f32[2,128,2048]{2,1,0:T(8,128)}, f32[2,128,2048]{2,1,0:T(8,128)}) custom-call(f32[256,4096]{1,0:T(8,128)} %get-tuple-element.77.keep2_ref.keep4_ref, f32[256,4096]{1,0:T(8,128)} %get-tuple-element.77.keep2_ref.keep4_ref, f32[256,4096]{1,0:T(8,128)} %collective-permute-done.17.got2_ref.got4_ref, ...), custom_call_target="tpu_custom_call" | custom-call | flops 2097152 | bytes 20971520 | tf_op jit(solution)/shard_map/second/pallas_call | solution.py:420
  341.0 1.5 collective-permute-start.24
  342.6 11.1 %collective-permute-done.16.x2a_ref = f32[128,2048]{1,0:T(8,128)} collective-permute-done((f32[128,2048]{1,0:T(8,128)}, f32[128,2048]{1,0:T(8,128)}, u32[]{:S(2)}, u32[]{:S(2)}) %collective-permute-start.16) | collective-permute-done | bytes 1048608 | tf_op jit(solution)/shard_map/ppermute | solution.py:479
  356.7 81.3 %dweight.1 = (f32[4016,4096]{1,0:T(8,128)}, f32[256,4096]{1,0:T(8,128)}) custom-call(bf16[4016,2048]{1,0:T(8,128)(2,1)} %get-tuple-element.72.dz_ref, f32[256,4096]{1,0:T(8,128)} %get-tuple-element.73.keep_ref, f32[256,4096]{1,0:T(8,128)} %collective-permute-done.15.got_ref, bf16[128,4096]{1,0:T(8,128)(2,1)} %get-tuple-element.50.refs_0_, ...), custom_call_target="tpu_custom_call" | custom-call | flops 67377299456 | bytes 98697216 | tf_op jit(solution)/shard_map/dweight/pallas_call | solution.py:232
  438.1 8.9 %last.1 = (bf16[256,4096]{1,0:T(8,128)(2,1)}, f32[8,512]{1,0:T(8,128)}) custom-call(bf16[256,4096]{1,0:T(8,128)(2,1)} %hid_ref.1, f32[1,4096]{1,0:T(1,128)} %bitcast.19, f32[256,4096]{1,0:T(8,128)} %get-tuple-element.75.q_ref, f32[128,2048]{1,0:T(8,128)} %collective-permute-done.16.x2a_ref, f32[128,2048]{1,0:T(8,128)} %collective-permute-done.21.x2b_ref, ...), custom_call_target="tpu_custom_call" | custom-call | flops 20971520 | bytes 20971520 | tf_op jit(solution)/shard_map/last/pallas_call | solution.py:463
  446.9 7.1 %shard_map.85 = (f32[32,128]{1,0:T(8,128)}, f32[1,1]{1,0:T(1,128)}) custom-call(f32[8,512]{1,0:T(8,128)} %get-tuple-element.90.gain_ref, f32[8,128]{1,0:T(8,128)} %get-tuple-element.91.loss_ref), custom_call_target="tpu_custom_call" | custom-call | flops 4000 | bytes 4000000 | tf_op jit(solution)/shard_map/pallas_call | solution.py:367
  (44 shorter events, 14.9 us)
Async XLA Ops:
  5.2 26.8 %collective-permute-start = (bf16[128,4096]{1,0:T(8,128)(2,1)}, bf16[128,4096]{1,0:T(8,128)(2,1)}, u32[]{:S(2)}, u32[]{:S(2)}) collective-permute-start(bf16[128,4096]{1,0:T(8,128)(2,1)} %get-tuple-element.50.refs_0_), channel_id=1, source_target_pairs={{0,2},{1,3},{2,0},{3,1},{4,6},{5,7},{6,4},{7,5},{8,10},{9,11},{10,... | collective-permute-start | bytes 3145736 | tf_op jit(solution)/shard_map/ppermute | solution.py:479
  7.7 26.3 %collective-permute-start.9 = (bf16[128,4096]{1,0:T(8,128)(2,1)}, bf16[128,4096]{1,0:T(8,128)(2,1)}, u32[]{:S(2)}, u32[]{:S(2)}) collective-permute-start(bf16[128,4096]{1,0:T(8,128)(2,1)} %get-tuple-element.50.refs_0_), channel_id=1, source_target_pairs={{0,4},{1,5},{2,6},{3,7},{4,0},{5,1},{6,2},{7,3},{8,12},{9,13},{10,... | collective-permute-start | bytes 3145736 | tf_op jit(solution)/shard_map/ppermute | solution.py:479
  9.2 26.4 %collective-permute-start.13 = (bf16[128,4096]{1,0:T(8,128)(2,1)}, bf16[128,4096]{1,0:T(8,128)(2,1)}, u32[]{:S(2)}, u32[]{:S(2)}) collective-permute-start(bf16[128,4096]{1,0:T(8,128)(2,1)} %get-tuple-element.51.refs_1_), channel_id=1, source_target_pairs={{0,1},{1,0},{2,3},{3,2},{4,5},{5,4},{6,7},{7,6},{8,9},{9,8},{10,11... | collective-permute-start | bytes 3145736 | tf_op jit(solution)/shard_map/ppermute | solution.py:479
  9.2 47.3 %collective-permute-start.2 = (bf16[128,4096]{1,0:T(8,128)(2,1)}, bf16[128,4096]{1,0:T(8,128)(2,1)}, u32[]{:S(2)}, u32[]{:S(2)}) collective-permute-start(bf16[128,4096]{1,0:T(8,128)(2,1)} %get-tuple-element.51.refs_1_), channel_id=1, source_target_pairs={{0,4},{1,5},{2,6},{3,7},{4,0},{5,1},{6,2},{7,3},{8,12},{9,13},{10,... | collective-permute-start | bytes 3145736 | tf_op jit(solution)/shard_map/ppermute | solution.py:479
  9.7 71.3 %collective-permute-start.6 = (bf16[128,4096]{1,0:T(8,128)(2,1)}, bf16[128,4096]{1,0:T(8,128)(2,1)}, u32[]{:S(2)}, u32[]{:S(2)}) collective-permute-start(bf16[128,4096]{1,0:T(8,128)(2,1)} %get-tuple-element.51.refs_1_), channel_id=1, source_target_pairs={{0,2},{1,3},{2,0},{3,1},{4,6},{5,7},{6,4},{7,5},{8,10},{9,11},{10,... | collective-permute-start | bytes 3145736 | tf_op jit(solution)/shard_map/ppermute | solution.py:479
  32.0 50.0 %collective-permute-start.10 = (bf16[128,4096]{1,0:T(8,128)(2,1)}, bf16[128,4096]{1,0:T(8,128)(2,1)}, u32[]{:S(2)}, u32[]{:S(2)}) collective-permute-start(bf16[128,4096]{1,0:T(8,128)(2,1)} %collective-permute-done.refs_0_.refs_4_), channel_id=1, source_target_pairs={{0,1},{1,0},{2,3},{3,2},{4,5},{5,4},{6,7},{7,6},{8,9},{9,8},{10,11... | collective-permute-start | bytes 3145736 | tf_op jit(solution)/shard_map/ppermute | solution.py:479
  34.0 47.5 %collective-permute-start.1 = (bf16[128,4096]{1,0:T(8,128)(2,1)}, bf16[128,4096]{1,0:T(8,128)(2,1)}, u32[]{:S(2)}, u32[]{:S(2)}) collective-permute-start(bf16[128,4096]{1,0:T(8,128)(2,1)} %collective-permute-done.refs_0_.refs_4_), channel_id=1, source_target_pairs={{0,4},{1,5},{2,6},{3,7},{4,0},{5,1},{6,2},{7,3},{8,12},{9,13},{10,... | collective-permute-start | bytes 3145736 | tf_op jit(solution)/shard_map/ppermute | solution.py:479
  35.5 45.5 %collective-permute-start.11 = (bf16[128,4096]{1,0:T(8,128)(2,1)}, bf16[128,4096]{1,0:T(8,128)(2,1)}, u32[]{:S(2)}, u32[]{:S(2)}) collective-permute-start(bf16[128,4096]{1,0:T(8,128)(2,1)} %collective-permute-done.9.refs_1_.refs_5_), channel_id=1, source_target_pairs={{0,1},{1,0},{2,3},{3,2},{4,5},{5,4},{6,7},{7,6},{8,9},{9,8},{10,11... | collective-permute-start | bytes 3145736 | tf_op jit(solution)/shard_map/ppermute | solution.py:479
  81.0 25.5 %collective-permute-start.8 = (bf16[128,4096]{1,0:T(8,128)(2,1)}, bf16[128,4096]{1,0:T(8,128)(2,1)}, u32[]{:S(2)}, u32[]{:S(2)}) collective-permute-start(bf16[128,4096]{1,0:T(8,128)(2,1)} %collective-permute-done.2.refs_1_.refs_9_), channel_id=1, source_target_pairs={{0,1},{1,0},{2,3},{3,2},{4,5},{5,4},{6,7},{7,6},{8,9},{9,8},{10,11... | collective-permute-start | bytes 3145736 | tf_op jit(solution)/shard_map/ppermute | solution.py:479
  81.0 25.5 %collective-permute-start.7 = (bf16[128,4096]{1,0:T(8,128)(2,1)}, bf16[128,4096]{1,0:T(8,128)(2,1)}, u32[]{:S(2)}, u32[]{:S(2)}) collective-permute-start(bf16[128,4096]{1,0:T(8,128)(2,1)} %collective-permute-done.6.refs_0_.refs_8_), channel_id=1, source_target_pairs={{0,1},{1,0},{2,3},{3,2},{4,5},{5,4},{6,7},{7,6},{8,9},{9,8},{10,11... | collective-permute-start | bytes 3145736 | tf_op jit(solution)/shard_map/ppermute | solution.py:479
  81.5 49.7 %collective-permute-start.4 = (bf16[128,4096]{1,0:T(8,128)(2,1)}, bf16[128,4096]{1,0:T(8,128)(2,1)}, u32[]{:S(2)}, u32[]{:S(2)}) collective-permute-start(bf16[128,4096]{1,0:T(8,128)(2,1)} %collective-permute-done.1.refs_0_.refs_12_), channel_id=1, source_target_pairs={{0,1},{1,0},{2,3},{3,2},{4,5},{5,4},{6,7},{7,6},{8,9},{9,8},{10,11... | collective-permute-start | bytes 3145736 | tf_op jit(solution)/shard_map/ppermute | solution.py:479
  81.6 49.6 %collective-permute-start.5 = (bf16[128,4096]{1,0:T(8,128)(2,1)}, bf16[128,4096]{1,0:T(8,128)(2,1)}, u32[]{:S(2)}, u32[]{:S(2)}) collective-permute-start(bf16[128,4096]{1,0:T(8,128)(2,1)} %collective-permute-done.3.refs_1_.refs_13_), channel_id=1, source_target_pairs={{0,1},{1,0},{2,3},{3,2},{4,5},{5,4},{6,7},{7,6},{8,9},{9,8},{10,11... | collective-permute-start | bytes 3145736 | tf_op jit(solution)/shard_map/ppermute | solution.py:479
  218.3 28.3 %collective-permute-start.14 = (f32[256,4096]{1,0:T(8,128)}, f32[256,4096]{1,0:T(8,128)}, u32[]{:S(2)}, u32[]{:S(2)}) collective-permute-start(f32[256,4096]{1,0:T(8,128)} %get-tuple-element.70), channel_id=1, source_target_pairs={{0,1},{1,0},{2,3},{3,2},{4,5},{5,4},{6,7},{7,6},{8,9},{9,8},{10,11... | collective-permute-start | bytes 12582920 | tf_op jit(solution)/shard_map/ppermute | solution.py:479
  218.4 58.3 %collective-permute-start.18 = (f32[256,4096]{1,0:T(8,128)}, f32[256,4096]{1,0:T(8,128)}, u32[]{:S(2)}, u32[]{:S(2)}) collective-permute-start(f32[256,4096]{1,0:T(8,128)} %get-tuple-element.82), channel_id=1, source_target_pairs={{0,1},{1,0},{2,3},{3,2},{4,5},{5,4},{6,7},{7,6},{8,9},{9,8},{10,11... | collective-permute-start | bytes 12582920 | tf_op jit(solution)/shard_map/ppermute | solution.py:479
  246.4 39.5 %collective-permute-start.17 = (f32[256,4096]{1,0:T(8,128)}, f32[256,4096]{1,0:T(8,128)}, u32[]{:S(2)}, u32[]{:S(2)}) collective-permute-start(f32[256,4096]{1,0:T(8,128)} %get-tuple-element.78), channel_id=1, source_target_pairs={{0,1},{1,0},{2,3},{3,2},{4,5},{5,4},{6,7},{7,6},{8,9},{9,8},{10,11... | collective-permute-start | bytes 12582920 | tf_op jit(solution)/shard_map/ppermute | solution.py:479
  276.2 79.0 %collective-permute-start.15 = (f32[256,4096]{1,0:T(8,128)}, f32[256,4096]{1,0:T(8,128)}, u32[]{:S(2)}, u32[]{:S(2)}) collective-permute-start(f32[256,4096]{1,0:T(8,128)} %get-tuple-element.74), channel_id=1, source_target_pairs={{0,1},{1,0},{2,3},{3,2},{4,5},{5,4},{6,7},{7,6},{8,9},{9,8},{10,11... | collective-permute-start | bytes 12582920 | tf_op jit(solution)/shard_map/ppermute | solution.py:479
  282.4 48.8 %collective-permute-start.19 = (f32[256,2048]{1,0:T(8,128)}, f32[256,2048]{1,0:T(8,128)}, u32[]{:S(2)}, u32[]{:S(2)}) collective-permute-start(f32[256,2048]{1,0:T(8,128)} %get-tuple-element.83), channel_id=1, source_target_pairs={{0,2},{1,3},{2,0},{3,1},{4,6},{5,7},{6,4},{7,5},{8,10},{9,11},{10,... | collective-permute-start | bytes 6291464 | tf_op jit(solution)/shard_map/ppermute | solution.py:479
  283.9 48.8 %collective-permute-start.20 = (f32[256,2048]{1,0:T(8,128)}, f32[256,2048]{1,0:T(8,128)}, u32[]{:S(2)}, u32[]{:S(2)}) collective-permute-start(f32[256,2048]{1,0:T(8,128)} %get-tuple-element.84), channel_id=1, source_target_pairs={{0,4},{1,5},{2,6},{3,7},{4,0},{5,1},{6,2},{7,3},{8,12},{9,13},{10,... | collective-permute-start | bytes 6291464 | tf_op jit(solution)/shard_map/ppermute | solution.py:479
  285.4 68.3 %collective-permute-start.16 = (f32[128,2048]{1,0:T(8,128)}, f32[128,2048]{1,0:T(8,128)}, u32[]{:S(2)}, u32[]{:S(2)}) collective-permute-start(f32[128,2048]{1,0:T(8,128)} %get-tuple-element.76), channel_id=1, source_target_pairs={{0,2},{1,3},{2,0},{3,1},{4,6},{5,7},{6,4},{7,5},{8,10},{9,11},{10,... | collective-permute-start | bytes 3145736 | tf_op jit(solution)/shard_map/ppermute | solution.py:479
  286.0 152.0 %collective-permute-start.23 = (f32[128,2048]{1,0:T(8,128)}, f32[128,2048]{1,0:T(8,128)}, u32[]{:S(2)}, u32[]{:S(2)}) collective-permute-start(f32[128,2048]{1,0:T(8,128)} %get-tuple-element.87), channel_id=1, source_target_pairs={{0,4},{1,5},{2,6},{3,7},{4,0},{5,1},{6,2},{7,3},{8,12},{9,13},{10,... | collective-permute-start | bytes 3145736 | tf_op jit(solution)/shard_map/ppermute | solution.py:479
  340.5 97.5 %collective-permute-start.21 = (f32[128,2048]{1,0:T(8,128)}, f32[128,2048]{1,0:T(8,128)}, u32[]{:S(2)}, u32[]{:S(2)}) collective-permute-start(f32[128,2048]{1,0:T(8,128)} %get-tuple-element.85), channel_id=1, source_target_pairs={{0,2},{1,3},{2,0},{3,1},{4,6},{5,7},{6,4},{7,5},{8,10},{9,11},{10,... | collective-permute-start | bytes 3145736 | tf_op jit(solution)/shard_map/ppermute | solution.py:479
  341.0 97.0 %collective-permute-start.24 = (f32[128,2048]{1,0:T(8,128)}, f32[128,2048]{1,0:T(8,128)}, u32[]{:S(2)}, u32[]{:S(2)}) collective-permute-start(f32[128,2048]{1,0:T(8,128)} %get-tuple-element.88), channel_id=1, source_target_pairs={{0,4},{1,5},{2,6},{3,7},{4,0},{5,1},{6,2},{7,3},{8,12},{9,13},{10,... | collective-permute-start | bytes 3145736 | tf_op jit(solution)/shard_map/ppermute | solution.py:479
  353.7 84.3 %collective-permute-start.22 = (f32[2,128,2048]{2,1,0:T(8,128)}, f32[2,128,2048]{2,1,0:T(8,128)}, u32[]{:S(2)}, u32[]{:S(2)}) collective-permute-start(f32[2,128,2048]{2,1,0:T(8,128)} %get-tuple-element.86), channel_id=1, source_target_pairs={{0,4},{1,5},{2,6},{3,7},{4,0},{5,1},{6,2},{7,3},{8,12},{9,13},{10,... | collective-permute-start | bytes 6291464 | tf_op jit(solution)/shard_map/ppermute | solution.py:479
  355.2 82.8 %collective-permute-start.25 = (f32[2,128,2048]{2,1,0:T(8,128)}, f32[2,128,2048]{2,1,0:T(8,128)}, u32[]{:S(2)}, u32[]{:S(2)}) collective-permute-start(f32[2,128,2048]{2,1,0:T(8,128)} %get-tuple-element.89), channel_id=1, source_target_pairs={{0,2},{1,3},{2,0},{3,1},{4,6},{5,7},{6,4},{7,5},{8,10},{9,11},{10,... | collective-permute-start | bytes 6291464 | tf_op jit(solution)/shard_map/ppermute | solution.py:479
  (2 other events, 30.3 us)
